TPU v7x, 32 devices: a whole 2x2x4 slice. The times are simulated.
32 devices in a mesh: section: 4 (over y, x), seq: 8 (over z, core).
Axes of the slice: x: 2, y: 2, z: 4, core: 2. Of those that a mesh axis runs over, the one named last changes fastest.
Arguments:
- queries: bfloat16 [4, 1024, 4096], P('section', 'seq'), may hold values from -500 to 500
- keys: bfloat16 [4, 1024, 512], P('section', 'seq'), may hold values from -6 to 6
- values: bfloat16 [4, 1024, 512], P('section', 'seq'), may hold values from -6 to 6
- out_grad: bfloat16 [4, 1024, 4096], P('section', 'seq'), may hold values from -6 to 6
- documents: int32 [4, 1024], P('section'), may hold values from 0 to 3, never falling along the last dimension, each value on 1 to 512 neighbouring positions
- query_weight: bfloat16 [4, 4096, 4096], P('section', 'seq'), may hold values from -0.09375 to 0.09375
- key_weight: bfloat16 [4, 512, 4096], P('section'), may hold values from -0.1875 to 0.1875
- value_weight: bfloat16 [4, 512, 4096], P('section'), may hold values from -0.1875 to 0.1875
Outputs:
- upstream: bfloat16 [4, 1024, 4096], P('section', 'seq')
Inputs may be any that keep to these rules, and one draw needn't show every extreme that they name: `documents`: each section's document ids never fall along its tokens.
All inputs are finite; a program needn't handle non-finite values.
Results may differ from a plain program's by a relative error of at most 0.0058.
Values may be sent and summed in bfloat16 or wider, within the bound.
A program may use at most 192 MiB of HBM per device.

v0:
```python
import functools
import math

import jax
import jax.numpy as jnp
from jax import lax
from jax.experimental import pallas as pl
from jax.experimental.pallas import tpu as pltpu
from jax.sharding import PartitionSpec as P

KV = 4
HD = 128
MESH = pl.DeviceIdType.MESH
F32 = jnp.float32
BF16 = jnp.bfloat16


def aligned(index, size):
    return pl.ds(pl.multiple_of(index * size, size), size)


def kernel(dims, q_in, k_in, v_in, o_in, ids_ref, wq_in, wk_in, wv_in, out_ref,
           q_all, o_all, k_all, v_all, k_turned, dk_sum, dv_sum, start_ref, grads, weights,
           right_buf, left_buf, acc, final,
           q_sent, o_sent, k_sent, v_sent, q_got, o_got, kv_got, kv_forwarded,
           w_local, w_sent, w_got, g_sent, g_got,
           right_sent, right_got, left_sent, left_got, final_sent, final_got):
    sections, count, tok, heads, width, cw = dims
    total = tok * count
    chips = count // 2
    rows = 2 * tok
    feats = heads * HD
    span = feats + 2 * HD
    half = width // 2
    chunks = half // cw
    scale = 1.0 / math.sqrt(HD)
    to_log2 = scale * math.log2(math.e)
    sec = lax.axis_index("section")
    me = lax.axis_index("seq")
    chip = me // 2
    core = me % 2
    partner = (sec, me + 1 - 2 * core)

    barrier = pltpu.get_barrier_semaphore()

    def greet(device):
        pl.semaphore_signal(barrier, inc=1, device_id=device, device_id_type=MESH)

    for off in range(1, count):
        greet((sec, lax.rem(me + off, count)))
    for p in range(2):
        @pl.when(sec > 0)
        def _():
            greet((sec - 1, 2 * chip + p))

        @pl.when(sec < sections - 1)
        def _():
            greet((sec + 1, 2 * chip + p))
    above = jnp.where(sec > 0, 2, 0)
    below = jnp.where(sec < sections - 1, 2, 0)
    pl.semaphore_wait(barrier, count - 1 + above + below)

    def remote(src, dst, send_sem, recv_sem, device):
        return pltpu.make_async_remote_copy(
            src_ref=src, dst_ref=dst, send_sem=send_sem, recv_sem=recv_sem,
            device_id=device, device_id_type=MESH)

    def kv_copies(peer):
        head = aligned(peer * KV // count, HD)
        mine = aligned(me, tok)
        return (remote(k_in.at[:, head], k_all.at[mine], k_sent.at[peer], kv_got.at[0, me],
                       (sec, peer)),
                remote(v_in.at[:, head], v_all.at[mine], v_sent.at[peer], kv_got.at[1, me],
                       (sec, peer)))

    def qo_copies(peer):
        cols = aligned(peer, feats)
        mine = aligned(core, tok)
        return (remote(q_in.at[:, cols], q_all.at[chip, mine], q_sent.at[peer],
                       q_got.at[chip], (sec, peer)),
                remote(o_in.at[:, cols], o_all.at[chip, mine], o_sent.at[peer],
                       o_got.at[chip], (sec, peer)))

    def w_copy():
        return remote(wq_in.at[:, aligned(1 - core, half)], weights.at[pl.ds(pl.multiple_of(core * span, HD), feats)],
                      w_sent.at[0], w_got.at[0], partner)

    def each_twin(act):
        for far in range(chips - 1, 0, -1):
            @pl.when(chip + far < chips)
            def _():
                act(me + 2 * far)

            @pl.when(chip >= far)
            def _():
                act(me - 2 * far)
        act(me + 1 - 2 * core)

    def each_peer(act):
        for far in range(chips - 1, 0, -1):
            for p in range(2):
                @pl.when(chip + far < chips)
                def _():
                    act(2 * (chip + far) + p)

                @pl.when(chip >= far)
                def _():
                    act(2 * (chip - far) + p)
        act(me + 1 - 2 * core)

    def start_both(copies):
        for copy in copies:
            copy.start()

    each_twin(lambda peer: start_both(kv_copies(peer)))
    each_peer(lambda peer: start_both(qo_copies(peer)))
    w_copy().start()

    mine = aligned(me, tok)
    own = aligned(me * KV // count, HD)
    pltpu.make_async_copy(k_in.at[:, own], k_all.at[mine], kv_got.at[0, me]).start()
    pltpu.make_async_copy(v_in.at[:, own], v_all.at[mine], kv_got.at[1, me]).start()
    own = aligned(me, feats)
    mine = aligned(core, tok)
    pltpu.make_async_copy(q_in.at[:, own], q_all.at[chip, mine], q_got.at[chip]).start()
    pltpu.make_async_copy(o_in.at[:, own], o_all.at[chip, mine], o_got.at[chip]).start()

    my_half = aligned(core, half)
    my_rows = pl.ds(pl.multiple_of(core * span, HD), feats)
    local = [pltpu.make_async_copy(wq_in.at[:, my_half], weights.at[my_rows], w_local.at[0])]
    for p in range(2):
        g = aligned((2 * chip + p) * KV // count, HD)
        base = p * span + feats
        local.append(pltpu.make_async_copy(
            wk_in.at[g, my_half], weights.at[base:base + HD], w_local.at[1 + p]))
        local.append(pltpu.make_async_copy(
            wv_in.at[g, my_half], weights.at[base + HD:base + 2 * HD], w_local.at[3 + p]))
    for copy in local:
        copy.start()

    @pl.when(sec == sections - 1)
    def _():
        out_ref[...] = jnp.zeros_like(out_ref)

    dk_sum[...] = jnp.zeros_like(dk_sum)
    dv_sum[...] = jnp.zeros_like(dv_sum)

    turned = jnp.broadcast_to(ids_ref[...], (HD, total)).T[:, :1]
    for b in range(chips):
        before = turned < ids_ref[:, b * rows:(b + 1) * rows]
        start_ref[:, b * rows:(b + 1) * rows] = jnp.sum(
            before.astype(jnp.int32), axis=0, keepdims=True)

    def forward(which, b):
        buf = (k_all, v_all)[which]
        part = buf.at[aligned(2 * b + core, tok)]
        return remote(part, part, kv_forwarded.at[which, b], kv_got.at[which, 2 * b + core],
                      partner)

    def kv_wait(which, source):
        part = (k_all, v_all)[which].at[aligned(source, tok)]
        pltpu.make_async_copy(part, part, kv_got.at[which, source]).wait()

    for b in range(chips):
        for which in range(2):
            kv_wait(which, 2 * b + core)

            @pl.when(chip != b)
            def _():
                forward(which, b).start()
    for b in range(chips):
        for which in range(2):
            kv_wait(which, 2 * b + 1 - core)
    k_turned[...] = k_all[...].T

    def grad_copy(b, p):
        here = grads.at[b * rows:(b + 1) * rows, pl.ds(pl.multiple_of(p * span, HD), span)]
        return remote(here, here, g_sent.at[b], g_got.at[b], partner)

    def attend(b):
        lo, hi = b * rows, (b + 1) * rows
        pltpu.make_async_copy(q_all.at[b], q_all.at[b], q_got.at[b]).wait()
        pltpu.make_async_copy(o_all.at[b], o_all.at[b], o_got.at[b]).wait()
        last = (((1,), (1,)), ((), ()))

        def one_head(h, carry):
            q = q_all[b, :, aligned(h, HD)]
            o = o_all[b, :, aligned(h, HD)]
            s = lax.dot_general(k_all[:hi], q, last, preferred_element_type=F32)
            dp = lax.dot_general(v_all[:hi], o, last, preferred_element_type=F32)
            j = lax.broadcasted_iota(jnp.int32, (hi, rows), 0)
            at = lax.broadcasted_iota(jnp.int32, (hi, rows), 1) + lo
            allowed = (j >= start_ref[:, lo:hi]) & (j <= at)
            s = jnp.where(allowed, s, -jnp.inf)
            top = jnp.max(s, axis=0, keepdims=True)
            e = jnp.exp2((s - top) * to_log2)
            inv = 1.0 / jnp.sum(e, axis=0, keepdims=True)
            delta = jnp.sum(e * dp, axis=0, keepdims=True) * inv
            p_low = (e * inv).astype(BF16)
            ds = (e * (dp - delta) * (inv * scale)).astype(BF16)
            dv_sum[:hi] += jnp.dot(p_low, o, preferred_element_type=F32)
            dk_sum[:hi] += jnp.dot(ds, q, preferred_element_type=F32)
            dq = jnp.dot(k_turned[:, :hi], ds, preferred_element_type=F32)
            col = pl.ds(pl.multiple_of(core * span + h * HD, HD), HD)
            grads[lo:hi, col] = dq.T.astype(BF16)
            return carry

        lax.fori_loop(0, heads, one_head, 0)
        tail = core * span + feats
        grads[lo:hi, pl.ds(pl.multiple_of(tail, HD), HD)] = dk_sum[lo:hi].astype(BF16)
        grads[lo:hi, pl.ds(pl.multiple_of(tail + HD, HD), HD)] = dv_sum[lo:hi].astype(BF16)
        grad_copy(b, core).start()

    def right_copy(d, k):
        here = right_buf.at[d, k]
        return remote(here, here, right_sent.at[d, k], right_got.at[d, k],
                      (sec, jnp.minimum(me + 2, count - 2 + core)))

    def left_copy(d, k):
        here = left_buf.at[d, k]
        return remote(here, here, left_sent.at[d, k], left_got.at[d, k],
                      (sec, jnp.maximum(me - 2, core)))

    def final_copy(k, p):
        return remote(final.at[k, p * tok:(p + 1) * tok],
                      out_ref.at[:, aligned(core * chunks + k, cw)],
                      final_sent.at[k, p], final_got.at[core, k],
                      (jnp.maximum(sec - 1, 0), 2 * chip + p))

    def product(d, k):
        return jnp.dot(grads[aligned(d, rows), :], weights[:, aligned(k, cw)],
                       preferred_element_type=F32)

    def set_out(d, buf, copy, first=0, end=None):
        def one(k, carry):
            buf[d, k] = product(d, k).astype(BF16)
            copy(d, k).start()
            return carry

        lax.fori_loop(first, chunks if end is None else end, one, 0)

    def pass_on(d, k, buf, copy):
        acc[...] = product(d, k)
        copy(d, k).wait_recv()
        buf[d, k] = (acc[...] + buf[d, k].astype(F32)).astype(BF16)
        copy(d, k).start()

    def finish(k):
        acc[...] = product(chip, k)

        @pl.when(chip > 0)
        def _():
            right_copy(chip, k).wait_recv()
            acc[...] += right_buf[chip, k].astype(F32)

        @pl.when(chip < chips - 1)
        def _():
            left_copy(chip, k).wait_recv()
            acc[...] += left_buf[chip, k].astype(F32)

        final[k] = acc[...].astype(BF16)

        @pl.when(sec > 0)
        def _():
            final_copy(k, 0).start()
            final_copy(k, 1).start()

    early = chunks - chunks * 3 // 8
    for b in range(chips - 1, -1, -1):
        attend(b)
        if b == chips - 1:
            for copy in local:
                copy.wait()
            other = pl.ds(pl.multiple_of((1 - core) * span, HD), feats)
            remote(wq_in.at[:, my_half], weights.at[other],
                   w_sent.at[0], w_got.at[0], partner).wait_recv()
        grad_copy(b, 1 - core).wait_recv()
        if b > 0:
            @pl.when(chip == 0)
            def _():
                set_out(b, right_buf, right_copy)
        if b < chips - 1:
            @pl.when(chip == chips - 1)
            def _():
                set_out(b, left_buf, left_copy, 0, early if b == chips - 2 else chunks)

    @pl.when(chip == chips - 1)
    def _():
        set_out(chips - 2, left_buf, left_copy, early, chunks)

    middle = (chip > 0) & (chip < chips - 1)

    @pl.when(middle)
    def _():
        def to_right(i, carry):
            pass_on(chips - 1 - i // chunks, i % chunks, right_buf, right_copy)
            return carry

        def to_left(i, carry):
            pass_on(chip - 1 - i // chunks, i % chunks, left_buf, left_copy)
            return carry

        lax.fori_loop(0, (chip - 1) * chunks, to_left, 0)
        lax.fori_loop(0, (chips - 1 - chip) * chunks, to_right, 0)

    def finish_one(k, carry):
        @pl.when(middle)
        def _():
            pass_on(0, k, left_buf, left_copy)

        @pl.when((chip != chips - 2) | (k < early))
        def _():
            finish(k)

        return carry

    lax.fori_loop(0, chunks, finish_one, 0)

    @pl.when(chip == chips - 2)
    def _():
        def one(k, carry):
            finish(k)
            return carry

        lax.fori_loop(early, chunks, one, 0)

    def sent_both(copies):
        for copy in copies:
            copy.wait_send()

    each_twin(lambda peer: sent_both(kv_copies(peer)))
    for b in range(chips):
        @pl.when(chip != b)
        def _():
            forward(0, b).wait_send()
            forward(1, b).wait_send()
    each_peer(lambda peer: sent_both(qo_copies(peer)))
    for b in range(chips):
        grad_copy(b, core).wait_send()
    w_copy().wait_send()

    def drain(k, carry):
        def right_done(i, c):
            right_copy(chips - 1 - i, k).wait_send()
            return c

        def left_done(i, c):
            left_copy(i, k).wait_send()
            return c

        lax.fori_loop(0, chips - 1 - chip, right_done, 0)
        lax.fori_loop(0, chip, left_done, 0)

        @pl.when(sec > 0)
        def _():
            final_copy(k, 0).wait_send()
            final_copy(k, 1).wait_send()

        @pl.when(sec < sections - 1)
        def _():
            for p in range(2):
                remote(final.at[k, :tok], out_ref.at[:, aligned(p * chunks + k, cw)],
                       final_sent.at[k, p], final_got.at[p, k], partner).wait_recv()

        return carry

    lax.fori_loop(0, chunks, drain, 0)


def body(queries, keys, values, out_grad, documents, query_weight, key_weight, value_weight):
    sections = lax.axis_size("section")
    count = lax.axis_size("seq")
    tok = queries.shape[1]
    total = tok * count
    feats = query_weight.shape[1]
    heads = feats // HD
    width = query_weight.shape[2]
    chips = count // 2
    rows = 2 * tok
    cw = min(256, width // 2)
    chunks = width // 2 // cw
    dma = pltpu.SemaphoreType.DMA
    deep = 2 * feats + 4 * HD
    anywhere = pl.BlockSpec(memory_space=pl.ANY)
    vmem = pl.BlockSpec(memory_space=pltpu.VMEM)
    out = pl.pallas_call(
        functools.partial(kernel, (sections, count, tok, heads, width, cw)),
        out_shape=jax.ShapeDtypeStruct((tok, width), BF16),
        in_specs=[anywhere] * 4 + [vmem] + [anywhere] * 3,
        out_specs=vmem,
        scratch_shapes=[
            pltpu.VMEM((chips, rows, feats), BF16),
            pltpu.VMEM((chips, rows, feats), BF16),
            pltpu.VMEM((total, HD), BF16),
            pltpu.VMEM((total, HD), BF16),
            pltpu.VMEM((HD, total), BF16),
            pltpu.VMEM((total, HD), F32),
            pltpu.VMEM((total, HD), F32),
            pltpu.VMEM((1, total), jnp.int32),
            pltpu.VMEM((total, deep), BF16),
            pltpu.VMEM((deep, width // 2), BF16),
            pltpu.VMEM((chips, chunks, rows, cw), BF16),
            pltpu.VMEM((chips, chunks, rows, cw), BF16),
            pltpu.VMEM((rows, cw), F32),
            pltpu.VMEM((chunks, rows, cw), BF16),
            dma((count,)),
            dma((count,)),
            dma((count,)),
            dma((count,)),
            dma((chips,)),
            dma((chips,)),
            dma((2, count)),
            dma((2, chips)),
            dma((5,)),
            dma((1,)),
            dma((1,)),
            dma((chips,)),
            dma((chips,)),
            dma((chips, chunks)),
            dma((chips, chunks)),
            dma((chips, chunks)),
            dma((chips, chunks)),
            dma((chunks, 2)),
            dma((2, chunks)),
        ],
        compiler_params=pltpu.CompilerParams(
            collective_id=0, has_side_effects=True, vmem_limit_bytes=62 * 1024 * 1024),
        name="attention_back",
    )(queries[0], keys[0], values[0], out_grad[0], documents,
      query_weight[0], key_weight[0], value_weight[0])
    return out[None]


def solution(mesh):
    in_specs = (
        P("section", "seq", None),
        P("section", "seq", None),
        P("section", "seq", None),
        P("section", "seq", None),
        P("section", None),
        P("section", "seq", None),
        P("section", None, None),
        P("section", None, None),
    )
    out_specs = P("section", "seq", None)
    return jax.shard_map(body, mesh=mesh, in_specs=in_specs, out_specs=out_specs, check_vma=False)
```

profile of v0, /device:TPU:1, one launch (start us, length us, event | category | flops | bytes accessed | tf_op | source)
XLA Modules:
  0.0 134.9 jit_solution(3780707453988796868)
XLA Ops:
  0.0 132.6 %attention_back.1 = bf16[128,4096]{1,0:T(8,128)(2,1)} custom-call(bf16[128,4096]{1,0:T(8,128)(2,1)} %bitcast.12, bf16[128,512]{1,0:T(8,128)(2,1)} %bitcast.14, bf16[128,512]{1,0:T(8,128)(2,1)} %bitcast.15, bf16[128,4096]{1,0:T(8,128)(2,1)} %bitcast.13, s32[1,1024]{1,0:T(1,128)} %ids_ref.1, bf16[512,4096]{1,0:T(8,128)(2,1)} %bitcast.8, ...), custom_call_target="tpu_custom_call" | custom-call | tf_op jit(solution)/shard_map/attention_back/pallas_call | solution.py:386
  132.7 2.3 %copy.10 = bf16[1,128,4096]{2,1,0:T(8,128)(2,1)} copy(bf16[1,128,4096]{2,1,0:T(8,128)(2,1)} %bitcast.11) | data formatting | bytes 2097152
where the time goes:
time: 135 us
  Pallas kernels  133 us (99%)
  local copies, waits for them, and re-layouts  2.29 us (2%)
    pallas_call x1, Pallas kernels, body(): pl.pallas_call(functools.partial(kernel, (sections, count, tok, heads, wi...  133 us

commit v1 on v0

v1 whole, which is shorter than its diff:
```python
import functools
import math

import jax
import jax.numpy as jnp
from jax import lax
from jax.experimental import pallas as pl
from jax.experimental.pallas import tpu as pltpu
from jax.sharding import PartitionSpec as P

HD = 128
MESH = pl.DeviceIdType.MESH
F32 = jnp.float32
BF16 = jnp.bfloat16


def aligned(index, size):
    return pl.ds(pl.multiple_of(index * size, size), size)


def kernel(dims, q_in, k_in, v_in, o_in, ids_ref, wq_in, wk_in, wv_in, out_ref,
           q_all, o_all, kv_all, k_turned, bias, dk_sum, dv_sum, dq_buf, grads, kv_grads,
           weights, kv_weights, right_buf, left_buf, acc, final,
           qo_sent, qo_got, kv_sent, kv_got, kv_passed, w_local, w_sent, w_got,
           dq_sent, g_got, kvg_sent, kvg_got,
           right_sent, right_got, left_sent, left_got, final_sent, final_got):
    sections, count, tok, heads, kv, width, cw, group, reach = dims
    chips = count // 2
    rows = 2 * tok
    feats = heads * HD
    chip_heads = 2 * heads
    own_heads = chips * heads
    half_feats = own_heads * HD
    kvh = kv // 2
    per = own_heads // kvh
    chunks = width // cw
    span = 2 * kvh * HD
    scale = 1.0 / math.sqrt(HD)
    to_log2 = scale * math.log2(math.e)
    sec = lax.axis_index("section")
    me = lax.axis_index("seq")
    chip = me // 2
    core = me % 2
    partner = (sec, me + 1 - 2 * core)
    last = chips - 1

    barrier = pltpu.get_barrier_semaphore()

    def greet(device):
        pl.semaphore_signal(barrier, inc=1, device_id=device, device_id_type=MESH)

    for off in range(1, count):
        greet((sec, lax.rem(me + off, count)))

    @pl.when(sec > 0)
    def _():
        greet((sec - 1, me))

    @pl.when(sec < sections - 1)
    def _():
        greet((sec + 1, me))

    above = jnp.where(sec > 0, 1, 0)
    below = jnp.where(sec < sections - 1, 1, 0)
    pl.semaphore_wait(barrier, count - 1 + above + below)

    def remote(src, dst, send_sem, recv_sem, device):
        return pltpu.make_async_remote_copy(
            src_ref=src, dst_ref=dst, send_sem=send_sem, recv_sem=recv_sem,
            device_id=device, device_id_type=MESH)

    kv_in = (k_in, v_in)
    right = jnp.minimum(chip + 1, last)

    def kv_head(half, g):
        return pl.ds(pl.multiple_of((half * kvh + g) * HD, HD), HD)

    def kv_right(which, g, p):
        return remote(kv_in[which].at[:, kv_head(p, g)],
                      kv_all.at[which, g, pl.ds(pl.multiple_of((reach - 1) * rows + core * tok, tok), tok)],
                      kv_sent.at[which, g, p], kv_got.at[which, g, 1, core], (sec, 2 * right + p))

    def kv_partner(which, g):
        return remote(kv_in[which].at[:, kv_head(1 - core, g)],
                      kv_all.at[which, g, pl.ds(pl.multiple_of(reach * rows + core * tok, tok), tok)],
                      kv_sent.at[which, g, 2], kv_got.at[which, g, 0, core], partner)

    def kv_own(which, g):
        return pltpu.make_async_copy(
            kv_in[which].at[:, kv_head(core, g)],
            kv_all.at[which, g, pl.ds(pl.multiple_of(reach * rows + core * tok, tok), tok)],
            kv_got.at[which, g, 0, core])

    def kv_block(which, g, e):
        return kv_all.at[which, g, pl.ds((reach - e) * rows, rows)]

    def kv_relay(which, g, e):
        return remote(kv_block(which, g, e), kv_block(which, g, e + 1),
                      kv_passed.at[which, g, e], kv_got.at[which, g, e + 1, 0],
                      (sec, 2 * right + core))

    def kv_wait(g, e):
        for which in range(2):
            if e < 2:
                for p in range(2):
                    part = kv_all.at[which, g, pl.ds((reach - e) * rows + p * tok, tok)]
                    pltpu.make_async_copy(part, part, kv_got.at[which, g, e, p]).wait()
            else:
                part = kv_block(which, g, e)
                pltpu.make_async_copy(part, part, kv_got.at[which, g, e, 0]).wait()

    def qo_partner(which):
        return remote((q_in, o_in)[which].at[:, aligned(1 - core, half_feats)],
                      (q_all, o_all)[which].at[aligned(core, tok)],
                      qo_sent.at[which], qo_got.at[which, 0], partner)

    def qo_own(which):
        return pltpu.make_async_copy((q_in, o_in)[which].at[:, aligned(core, half_feats)],
                                     (q_all, o_all)[which].at[aligned(core, tok)],
                                     qo_got.at[which, 1])

    w_copy = remote(wq_in, weights.at[aligned(core, feats)], w_sent.at[0], w_got.at[0], partner)

    @pl.when(chip < last)
    def _():
        for g in range(kvh):
            for which in range(2):
                for p in range(2):
                    kv_right(which, g, p).start()

    for g in range(kvh):
        for which in range(2):
            kv_own(which, g).start()
            kv_partner(which, g).start()
    for which in range(2):
        qo_own(which).start()
        qo_partner(which).start()

    w_copy.start()
    local = [pltpu.make_async_copy(wq_in, weights.at[aligned(core, feats)], w_local.at[0])]
    for r in range(2):
        part = slice(r * kvh * HD, (r + 1) * kvh * HD)
        for which, source in enumerate((wk_in, wv_in)):
            base = r * span + which * kvh * HD
            local.append(pltpu.make_async_copy(
                source.at[part], kv_weights.at[base:base + kvh * HD],
                w_local.at[1 + 2 * r + which]))
    for copy in local:
        copy.start()

    @pl.when(sec == sections - 1)
    def _():
        out_ref[...] = jnp.zeros_like(out_ref)

    q_ids = ids_ref[:, aligned(chip, rows)]

    def set_bias(blocks):
        here = blocks * rows
        first = pl.ds(pl.multiple_of((chip + 1 - blocks) * rows, rows), here)
        k_ids = jnp.broadcast_to(ids_ref[:, first], (HD, here)).T[:, :1]
        same = k_ids == q_ids
        j = lax.broadcasted_iota(jnp.int32, (here, rows), 0)
        i = lax.broadcasted_iota(jnp.int32, (here, rows), 1) + (blocks - 1) * rows
        bias[:here] = jnp.where(same & (j <= i), 0.0, -jnp.inf)

    for blocks in range(1, reach + 2):
        @pl.when(jnp.minimum(chip, reach) + 1 == blocks)
        def _():
            set_bias(blocks)

    for e in range(1, reach):
        @pl.when((chip >= e) & (chip < last))
        def _():
            for g in range(kvh):
                kv_wait(g, e)
                for which in range(2):
                    kv_relay(which, g, e).start()

    for which in range(2):
        buf = (q_all, o_all)[which]
        qo_own(which).wait()
        part = buf.at[aligned(1 - core, tok)]
        pltpu.make_async_copy(part, part, qo_got.at[which, 0]).wait()

    def dq_place(unit):
        head = unit * group
        target = core * (chips // 2) + head // chip_heads
        piece = (head % chip_heads) // group
        return target, piece

    def dq_copy(unit, p):
        target, piece = dq_place(unit)
        return remote(dq_buf.at[unit, p * tok:(p + 1) * tok],
                      grads.at[chip, :, aligned(piece, group * HD)],
                      dq_sent.at[unit, p], g_got.at[chip, piece], (sec, 2 * target + p))

    def dq_out(unit):
        target, piece = dq_place(unit)
        for p in range(2):
            @pl.when(2 * target + p != me)
            def _():
                dq_copy(unit, p).start()

            @pl.when(2 * target + p == me)
            def _():
                grads[chip, :, aligned(piece, group * HD)] = dq_buf[unit, p * tok:(p + 1) * tok]

    dims_last = (((1,), (1,)), ((), ()))

    def attend(blocks):
        here = blocks * rows
        low = (reach + 1 - blocks) * rows
        for g in range(kvh):
            for e in range(blocks):
                if 1 <= e < reach:
                    @pl.when(chip == last)
                    def _():
                        kv_wait(g, e)
                else:
                    kv_wait(g, e)
            k_turned[:, :here] = kv_all[0, g, low:].T
            dk_sum[:here] = jnp.zeros((here, HD), F32)
            dv_sum[:here] = jnp.zeros((here, HD), F32)

            def one_unit(n, carry):
                unit = g * (per // group) + n
                dk = jnp.zeros((here, HD), F32)
                dv = jnp.zeros((here, HD), F32)
                for h in range(group):
                    col = aligned(unit * group + h, HD)
                    q = q_all[:, col]
                    o = o_all[:, col]
                    s = lax.dot_general(kv_all[0, g, low:], q, dims_last, preferred_element_type=F32)
                    dp = lax.dot_general(kv_all[1, g, low:], o, dims_last, preferred_element_type=F32)
                    s = s + bias[:here]
                    top = jnp.max(s, axis=0, keepdims=True)
                    e = jnp.exp2((s - top) * to_log2)
                    inv = 1.0 / jnp.sum(e, axis=0, keepdims=True)
                    delta = jnp.sum(e * dp, axis=0, keepdims=True) * inv
                    prob = e * inv
                    ds = (prob * (dp - delta)).astype(BF16)
                    dv += jnp.dot(prob.astype(BF16), o, preferred_element_type=F32)
                    dk += jnp.dot(ds, q, preferred_element_type=F32)
                    dq = jnp.dot(k_turned[:, :here], ds, preferred_element_type=F32) * scale
                    dq_buf[unit, :, h * HD:(h + 1) * HD] = dq.T.astype(BF16)
                dk_sum[:here] += dk
                dv_sum[:here] += dv
                dq_out(unit)
                return carry

            lax.fori_loop(0, per // group, one_unit, 0)
            for e in range(blocks):
                at = (blocks - 1 - e) * rows
                for which, sums in enumerate((dk_sum, dv_sum)):
                    col = aligned(core * 2 * kvh + which * kvh + g, HD)
                    for p in range(2):
                        part = sums[at + p * tok:at + (p + 1) * tok]
                        if which == 0:
                            part = part * scale
                        kv_grads[e, p, :, col] = part.astype(BF16)

    def kvg_copy(e):
        part = kv_grads.at[e, 1 - core, :, aligned(core, span)]
        return remote(part, part, kvg_sent.at[e], kvg_got.at[e], partner)

    for blocks in range(1, reach + 2):
        @pl.when(jnp.minimum(chip, reach) + 1 == blocks)
        def _():
            attend(blocks)
            for e in range(blocks):
                kvg_copy(e).start()
            if blocks == 1:
                for copy in local:
                    copy.wait()
                part = weights.at[aligned(1 - core, feats)]
                pltpu.make_async_copy(part, part, w_got.at[0]).wait()
            else:
                for copy in local:
                    copy.wait()
                part = weights.at[aligned(1 - core, feats)]
                pltpu.make_async_copy(part, part, w_got.at[0]).wait()

    def kvg_wait(e):
        part = kv_grads.at[e, core, :, aligned(1 - core, span)]
        pltpu.make_async_copy(part, part, kvg_got.at[e]).wait()

    for e in range(reach + 1):
        @pl.when(chip >= e)
        def _():
            kvg_wait(e)

    def grads_wait(b):
        for piece in range(chip_heads // group):
            part = grads.at[b, :, piece * group * HD:(piece + 1) * group * HD]
            pltpu.make_async_copy(part, part, g_got.at[b, piece]).wait()

    for b in range(chips):
        @pl.when((chip == b) & (b // (chips // 2) != core))
        def _():
            grads_wait(b)

    def right_copy(d, k):
        here = right_buf.at[d, k]
        return remote(here, here, right_sent.at[d, k], right_got.at[d, k],
                      (sec, jnp.minimum(me + 2, count - 2 + core)))

    def left_copy(d, k):
        here = left_buf.at[d, k]
        return remote(here, here, left_sent.at[d, k], left_got.at[d, k],
                      (sec, jnp.maximum(me - 2, core)))

    def final_copy(k):
        return remote(final.at[k], out_ref.at[:, aligned(k, cw)], final_sent.at[k], final_got.at[k],
                      (jnp.maximum(sec - 1, 0), me))

    def product(d, k):
        acc[...] = jnp.dot(grads[d], weights[:, aligned(k, cw)], preferred_element_type=F32)

    def kv_product(e, k):
        acc[...] += jnp.dot(kv_grads[e, core], kv_weights[:, aligned(k, cw)],
                            preferred_element_type=F32)

    def pass_right(d, k):
        product(d, k)

        @pl.when(chip > 0)
        def _():
            right_copy(d, k).wait_recv()
            acc[...] += right_buf[d, k].astype(F32)

        right_buf[d, k] = acc[...].astype(BF16)
        right_copy(d, k).start()

    def pass_left(d, k):
        product(d, k)

        @pl.when(chip - d <= reach)
        def _():
            kv_product(jnp.minimum(chip - d, reach), k)

        @pl.when(chip < last)
        def _():
            left_copy(d, k).wait_recv()
            acc[...] += left_buf[d, k].astype(F32)

        left_buf[d, k] = acc[...].astype(BF16)
        left_copy(d, k).start()

    def finish(k):
        product(chip, k)
        kv_product(0, k)

        @pl.when(chip > 0)
        def _():
            right_copy(chip, k).wait_recv()
            acc[...] += right_buf[chip, k].astype(F32)

        @pl.when(chip < last)
        def _():
            left_copy(chip, k).wait_recv()
            acc[...] += left_buf[chip, k].astype(F32)

        final[k] = acc[...].astype(BF16)

        @pl.when(sec > 0)
        def _():
            final_copy(k).start()

    def each(first, end, act):
        def one(k, carry):
            act(k)
            return carry

        lax.fori_loop(first, end, one, 0)

    early = chunks * 3 // 8 if chips > 2 else 0

    if early:
        @pl.when(chip == 0)
        def _():
            grads_wait(1)
            each(0, early, lambda k: pass_right(1, k))

    for i in range(chips - 1):
        far, near = chips - 1 - i, i
        to_right = chip < far
        to_left = chip > near
        begin = early if i == chips - 2 else 0

        @pl.when(to_right)
        def _():
            if begin == 0:
                grads_wait(far)

        @pl.when(to_left)
        def _():
            grads_wait(near)

        def one(k):
            if begin == 0:
                @pl.when(to_right)
                def _():
                    pass_right(far, k)
            else:
                @pl.when(to_right & (k >= begin))
                def _():
                    pass_right(far, k)

            @pl.when(to_left)
            def _():
                pass_left(near, k)

            if i == 1 and early:
                @pl.when((chip == 1) & (k < early))
                def _():
                    finish(k)

        each(0, chunks, one)

    each(0, early, lambda k: pl.when(chip != 1)(lambda: finish(k)))
    each(early, chunks, finish)

    @pl.when(chip < last)
    def _():
        for g in range(kvh):
            for which in range(2):
                for p in range(2):
                    kv_right(which, g, p).wait_send()

    for e in range(1, reach):
        @pl.when((chip >= e) & (chip < last))
        def _():
            for g in range(kvh):
                for which in range(2):
                    kv_relay(which, g, e).wait_send()

    for which in range(2):
        for g in range(kvh):
            kv_partner(which, g).wait_send()
        qo_partner(which).wait_send()
    w_copy.wait_send()

    def dq_done(unit, carry):
        target, _ = dq_place(unit)
        for p in range(2):
            @pl.when(2 * target + p != me)
            def _():
                dq_copy(unit, p).wait_send()
        return carry

    lax.fori_loop(0, own_heads // group, dq_done, 0)

    for e in range(reach + 1):
        @pl.when(chip >= e)
        def _():
            kvg_copy(e).wait_send()

    def drain(k):
        def right_done(i, c):
            right_copy(last - i, k).wait_send()
            return c

        def left_done(i, c):
            left_copy(i, k).wait_send()
            return c

        lax.fori_loop(0, last - chip, right_done, 0)
        lax.fori_loop(0, chip, left_done, 0)

        @pl.when(sec > 0)
        def _():
            final_copy(k).wait_send()

        @pl.when(sec < sections - 1)
        def _():
            final_copy(k).wait_recv()

    each(0, chunks, drain)


def body(queries, keys, values, out_grad, documents, query_weight, key_weight, value_weight):
    sections = lax.axis_size("section")
    count = lax.axis_size("seq")
    tok = queries.shape[1]
    total = tok * count
    kv = keys.shape[2] // HD
    feats = query_weight.shape[1]
    heads = feats // HD
    width = query_weight.shape[2]
    chips = count // 2
    rows = 2 * tok
    reach = -(-(total // 2) // rows)
    group = 2
    cw = min(512, width)
    chunks = width // cw
    units = chips * heads // group
    kvh = kv // 2
    slots = (reach + 1) * rows
    dma = pltpu.SemaphoreType.DMA
    anywhere = pl.BlockSpec(memory_space=pl.ANY)
    vmem = pl.BlockSpec(memory_space=pltpu.VMEM)
    out = pl.pallas_call(
        functools.partial(kernel, (sections, count, tok, heads, kv, width, cw, group, reach)),
        out_shape=jax.ShapeDtypeStruct((tok, width), BF16),
        in_specs=[anywhere] * 4 + [vmem] + [anywhere] * 3,
        out_specs=vmem,
        scratch_shapes=[
            pltpu.VMEM((rows, chips * feats), BF16),
            pltpu.VMEM((rows, chips * feats), BF16),
            pltpu.VMEM((2, kvh, slots, HD), BF16),
            pltpu.VMEM((HD, slots), BF16),
            pltpu.VMEM((slots, rows), F32),
            pltpu.VMEM((slots, HD), F32),
            pltpu.VMEM((slots, HD), F32),
            pltpu.VMEM((units, rows, group * HD), BF16),
            pltpu.VMEM((chips, tok, 2 * feats), BF16),
            pltpu.VMEM((reach + 1, 2, tok, 2 * kv * HD), BF16),
            pltpu.VMEM((2 * feats, width), BF16),
            pltpu.VMEM((2 * kv * HD, width), BF16),
            pltpu.VMEM((chips, chunks, tok, cw), BF16),
            pltpu.VMEM((chips, chunks, tok, cw), BF16),
            pltpu.VMEM((tok, cw), F32),
            pltpu.VMEM((chunks, tok, cw), BF16),
            dma((2,)),
            dma((2, 2)),
            dma((2, kvh, 3)),
            dma((2, kvh, reach + 1, 2)),
            dma((2, kvh, reach + 1)),
            dma((5,)),
            dma((1,)),
            dma((1,)),
            dma((units, 2)),
            dma((chips, 2 * heads // group)),
            dma((reach + 1,)),
            dma((reach + 1,)),
            dma((chips, chunks)),
            dma((chips, chunks)),
            dma((chips, chunks)),
            dma((chips, chunks)),
            dma((chunks,)),
            dma((chunks,)),
        ],
        compiler_params=pltpu.CompilerParams(
            collective_id=0, has_side_effects=True, vmem_limit_bytes=62 * 1024 * 1024),
        name="attention_back",
    )(queries[0], keys[0], values[0], out_grad[0], documents,
      query_weight[0], key_weight[0], value_weight[0])
    return out[None]


def solution(mesh):
    in_specs = (
        P("section", "seq", None),
        P("section", "seq", None),
        P("section", "seq", None),
        P("section", "seq", None),
        P("section", None),
        P("section", "seq", None),
        P("section", None, None),
        P("section", None, None),
    )
    out_specs = P("section", "seq", None)
    return jax.shard_map(body, mesh=mesh, in_specs=in_specs, out_specs=out_specs, check_vma=False)
```

time: 135 us -> 145 us (1.074)
  the two profiles are of different devices: /device:TPU:1 before, /device:TPU:20 now
where the time goes in v1:
time: 145 us; the launch traced here: 144 us
  Pallas kernels  142 us (98%)
  local copies, waits for them, and re-layouts  2.29 us (2%)
    pallas_call x1, Pallas kernels, body(): pl.pallas_call(functools.partial(kernel, (sections, count, tok, heads, kv...  142 us

profile of v1, /device:TPU:20, one launch (start us, length us, event | category | flops | bytes accessed | tf_op | source)
XLA Modules:
  0.0 144.5 jit_solution(15741227747216426448)
XLA Ops:
  0.0 142.2 %attention_back.1 = bf16[128,4096]{1,0:T(8,128)(2,1)} custom-call(bf16[128,4096]{1,0:T(8,128)(2,1)} %bitcast.12, bf16[128,512]{1,0:T(8,128)(2,1)} %bitcast.14, bf16[128,512]{1,0:T(8,128)(2,1)} %bitcast.15, bf16[128,4096]{1,0:T(8,128)(2,1)} %bitcast.13, s32[1,1024]{1,0:T(1,128)} %ids_ref.1, bf16[512,4096]{1,0:T(8,128)(2,1)} %bitcast.8, ...), custom_call_target="tpu_custom_call" | custom-call | tf_op jit(solution)/shard_map/attention_back/pallas_call | solution.py:502
  142.2 2.3 %copy.10 = bf16[1,128,4096]{2,1,0:T(8,128)(2,1)} copy(bf16[1,128,4096]{2,1,0:T(8,128)(2,1)} %bitcast.11) | data formatting | bytes 2097152

commit v2 on v1

--- a/solution.py
+++ b/solution.py
@@ -62,7 +62,8 @@
 
     above = jnp.where(sec > 0, 1, 0)
     below = jnp.where(sec < sections - 1, 1, 0)
-    pl.semaphore_wait(barrier, count - 1 + above + below)
+    with jax.named_scope('barrier'):
+        pl.semaphore_wait(barrier, count - 1 + above + below)
 
     def remote(src, dst, send_sem, recv_sem, device):
         return pltpu.make_async_remote_copy(
@@ -166,21 +167,24 @@
     for blocks in range(1, reach + 2):
         @pl.when(jnp.minimum(chip, reach) + 1 == blocks)
         def _():
-            set_bias(blocks)
+            with jax.named_scope('bias'):
+                set_bias(blocks)
 
     for e in range(1, reach):
         @pl.when((chip >= e) & (chip < last))
         def _():
-            for g in range(kvh):
-                kv_wait(g, e)
-                for which in range(2):
-                    kv_relay(which, g, e).start()
-
-    for which in range(2):
-        buf = (q_all, o_all)[which]
-        qo_own(which).wait()
-        part = buf.at[aligned(1 - core, tok)]
-        pltpu.make_async_copy(part, part, qo_got.at[which, 0]).wait()
+            with jax.named_scope('relay'):
+                for g in range(kvh):
+                    kv_wait(g, e)
+                    for which in range(2):
+                        kv_relay(which, g, e).start()
+
+    with jax.named_scope('qo_wait'):
+        for which in range(2):
+            buf = (q_all, o_all)[which]
+            qo_own(which).wait()
+            part = buf.at[aligned(1 - core, tok)]
+            pltpu.make_async_copy(part, part, qo_got.at[which, 0]).wait()
 
     def dq_place(unit):
         head = unit * group
@@ -211,13 +215,14 @@
         here = blocks * rows
         low = (reach + 1 - blocks) * rows
         for g in range(kvh):
-            for e in range(blocks):
-                if 1 <= e < reach:
-                    @pl.when(chip == last)
-                    def _():
+            with jax.named_scope('kv_wait'):
+                for e in range(blocks):
+                    if 1 <= e < reach:
+                        @pl.when(chip == last)
+                        def _():
+                            kv_wait(g, e)
+                    else:
                         kv_wait(g, e)
-                else:
-                    kv_wait(g, e)
             k_turned[:, :here] = kv_all[0, g, low:].T
             dk_sum[:here] = jnp.zeros((here, HD), F32)
             dv_sum[:here] = jnp.zeros((here, HD), F32)
@@ -248,7 +253,8 @@
                 dq_out(unit)
                 return carry
 
-            lax.fori_loop(0, per // group, one_unit, 0)
+            with jax.named_scope('attend'):
+                lax.fori_loop(0, per // group, one_unit, 0)
             for e in range(blocks):
                 at = (blocks - 1 - e) * rows
                 for which, sums in enumerate((dk_sum, dv_sum)):
@@ -269,30 +275,28 @@
             attend(blocks)
             for e in range(blocks):
                 kvg_copy(e).start()
-            if blocks == 1:
-                for copy in local:
-                    copy.wait()
-                part = weights.at[aligned(1 - core, feats)]
-                pltpu.make_async_copy(part, part, w_got.at[0]).wait()
-            else:
-                for copy in local:
-                    copy.wait()
-                part = weights.at[aligned(1 - core, feats)]
-                pltpu.make_async_copy(part, part, w_got.at[0]).wait()
 
     def kvg_wait(e):
         part = kv_grads.at[e, core, :, aligned(1 - core, span)]
         pltpu.make_async_copy(part, part, kvg_got.at[e]).wait()
 
-    for e in range(reach + 1):
-        @pl.when(chip >= e)
-        def _():
-            kvg_wait(e)
+    with jax.named_scope('w_wait'):
+        for copy in local:
+            copy.wait()
+        theirs = weights.at[aligned(1 - core, feats)]
+        pltpu.make_async_copy(theirs, theirs, w_got.at[0]).wait()
+
+    with jax.named_scope('kvg_wait'):
+        for e in range(reach + 1):
+            @pl.when(chip >= e)
+            def _():
+                kvg_wait(e)
 
     def grads_wait(b):
-        for piece in range(chip_heads // group):
-            part = grads.at[b, :, piece * group * HD:(piece + 1) * group * HD]
-            pltpu.make_async_copy(part, part, g_got.at[b, piece]).wait()
+        with jax.named_scope('g_wait'):
+            for piece in range(chip_heads // group):
+                part = grads.at[b, :, piece * group * HD:(piece + 1) * group * HD]
+                pltpu.make_async_copy(part, part, g_got.at[b, piece]).wait()
 
     for b in range(chips):
         @pl.when((chip == b) & (b // (chips // 2) != core))
@@ -321,43 +325,50 @@
                             preferred_element_type=F32)
 
     def pass_right(d, k):
-        product(d, k)
+        with jax.named_scope('r_prod'):
+            product(d, k)
 
         @pl.when(chip > 0)
         def _():
-            right_copy(d, k).wait_recv()
+            with jax.named_scope('r_wait'):
+                right_copy(d, k).wait_recv()
             acc[...] += right_buf[d, k].astype(F32)
 
         right_buf[d, k] = acc[...].astype(BF16)
         right_copy(d, k).start()
 
     def pass_left(d, k):
-        product(d, k)
-
-        @pl.when(chip - d <= reach)
-        def _():
-            kv_product(jnp.minimum(chip - d, reach), k)
+        with jax.named_scope('l_prod'):
+            product(d, k)
+
+            @pl.when(chip - d <= reach)
+            def _():
+                kv_product(jnp.minimum(chip - d, reach), k)
 
         @pl.when(chip < last)
         def _():
-            left_copy(d, k).wait_recv()
+            with jax.named_scope('l_wait'):
+                left_copy(d, k).wait_recv()
             acc[...] += left_buf[d, k].astype(F32)
 
         left_buf[d, k] = acc[...].astype(BF16)
         left_copy(d, k).start()
 
     def finish(k):
-        product(chip, k)
-        kv_product(0, k)
+        with jax.named_scope('f_prod'):
+            product(chip, k)
+            kv_product(0, k)
 
         @pl.when(chip > 0)
         def _():
-            right_copy(chip, k).wait_recv()
+            with jax.named_scope('f_wait_r'):
+                right_copy(chip, k).wait_recv()
             acc[...] += right_buf[chip, k].astype(F32)
 
         @pl.when(chip < last)
         def _():
-            left_copy(chip, k).wait_recv()
+            with jax.named_scope('f_wait_l'):
+                left_copy(chip, k).wait_recv()
             acc[...] += left_buf[chip, k].astype(F32)
 
         final[k] = acc[...].astype(BF16)
@@ -374,6 +385,8 @@
         lax.fori_loop(first, end, one, 0)
 
     early = chunks * 3 // 8 if chips > 2 else 0
+    lag = 3
+    leads_right = chip < chips // 2
 
     if early:
         @pl.when(chip == 0)
@@ -396,26 +409,24 @@
         def _():
             grads_wait(near)
 
-        def one(k):
-            if begin == 0:
-                @pl.when(to_right)
+        def one(step):
+            k_right = step - jnp.where(leads_right, 0, lag)
+            k_left = step - jnp.where(leads_right, lag, 0)
+
+            @pl.when(to_right & (k_right >= begin) & (k_right < chunks))
+            def _():
+                pass_right(far, k_right)
+
+            @pl.when(to_left & (k_left >= 0) & (k_left < chunks))
+            def _():
+                pass_left(near, k_left)
+
+            if i == 1 and early:
+                @pl.when((chip == 1) & (k_left >= 0) & (k_left < early))
                 def _():
-                    pass_right(far, k)
-            else:
-                @pl.when(to_right & (k >= begin))
-                def _():
-                    pass_right(far, k)
-
-            @pl.when(to_left)
-            def _():
-                pass_left(near, k)
-
-            if i == 1 and early:
-                @pl.when((chip == 1) & (k < early))
-                def _():
-                    finish(k)
-
-        each(0, chunks, one)
+                    finish(k_left)
+
+        each(0, chunks + lag, one)
 
     each(0, early, lambda k: pl.when(chip != 1)(lambda: finish(k)))
     each(early, chunks, finish)
@@ -475,7 +486,8 @@
         def _():
             final_copy(k).wait_recv()
 
-    each(0, chunks, drain)
+    with jax.named_scope('drain'):
+        each(0, chunks, drain)
 
 
 def body(queries, keys, values, out_grad, documents, query_weight, key_weight, value_weight):

time: 145 us -> 114 us (0.79)
  Pallas kernels: 142 us -> 111 us
    pallas_call x1, Pallas kernels: 142 us -> 111 us  [body(): pl.pallas_call(functools.partial(kernel, (sections, count, tok, heads, kv...]
where the time goes in v2:
time: 114 us; the launch traced here: 113 us
  Pallas kernels  111 us (97%)
  local copies, waits for them, and re-layouts  2.29 us (2%)
    pallas_call x1, Pallas kernels, body(): pl.pallas_call(functools.partial(kernel, (sections, count, tok, heads, kv...  111 us
    unnamed x1, local copies, waits for them, and re-layouts  2.29 us

profile of v2, /device:TPU:20, one launch (start us, length us, event | category | flops | bytes accessed | tf_op | source)
XLA Modules:
  0.0 113.4 jit_solution(16875775627372684424)
XLA Ops:
  0.0 111.1 %attention_back.1 = bf16[128,4096]{1,0:T(8,128)(2,1)} custom-call(bf16[128,4096]{1,0:T(8,128)(2,1)} %bitcast.12, bf16[128,512]{1,0:T(8,128)(2,1)} %bitcast.14, bf16[128,512]{1,0:T(8,128)(2,1)} %bitcast.15, bf16[128,4096]{1,0:T(8,128)(2,1)} %bitcast.13, s32[1,1024]{1,0:T(1,128)} %ids_ref.1, bf16[512,4096]{1,0:T(8,128)(2,1)} %bitcast.8, ...), custom_call_target="tpu_custom_call" | custom-call | tf_op jit(solution)/shard_map/attention_back/pallas_call | solution.py:514
  111.1 2.3 %copy.10 = bf16[1,128,4096]{2,1,0:T(8,128)(2,1)} copy(bf16[1,128,4096]{2,1,0:T(8,128)(2,1)} %bitcast.11) | data formatting | bytes 2097152

commit v3 on v2

--- a/solution.py
+++ b/solution.py
@@ -30,6 +30,7 @@
     feats = heads * HD
     chip_heads = 2 * heads
     own_heads = chips * heads
+    units = own_heads // group
     half_feats = own_heads * HD
     kvh = kv // 2
     per = own_heads // kvh
@@ -79,36 +80,41 @@
     def kv_right(which, g, p):
         return remote(kv_in[which].at[:, kv_head(p, g)],
                       kv_all.at[which, g, pl.ds(pl.multiple_of((reach - 1) * rows + core * tok, tok), tok)],
-                      kv_sent.at[which, g, p], kv_got.at[which, g, 1, core], (sec, 2 * right + p))
+                      kv_sent.at[0], kv_got.at[which, g, 1], (sec, 2 * right + p))
+
+    def kv_direct(which, g, p):
+        return remote(kv_in[which].at[:, kv_head(p, g)],
+                      kv_all.at[which, g, pl.ds(pl.multiple_of((reach - 2) * rows + core * tok, tok), tok)],
+                      kv_sent.at[0], kv_got.at[which, g, 2], (sec, 2 * last + p))
 
     def kv_partner(which, g):
         return remote(kv_in[which].at[:, kv_head(1 - core, g)],
                       kv_all.at[which, g, pl.ds(pl.multiple_of(reach * rows + core * tok, tok), tok)],
-                      kv_sent.at[which, g, 2], kv_got.at[which, g, 0, core], partner)
+                      kv_sent.at[0], kv_got.at[which, g, 0], partner)
 
     def kv_own(which, g):
         return pltpu.make_async_copy(
             kv_in[which].at[:, kv_head(core, g)],
             kv_all.at[which, g, pl.ds(pl.multiple_of(reach * rows + core * tok, tok), tok)],
-            kv_got.at[which, g, 0, core])
+            kv_got.at[which, g, 0])
 
     def kv_block(which, g, e):
         return kv_all.at[which, g, pl.ds((reach - e) * rows, rows)]
 
     def kv_relay(which, g, e):
         return remote(kv_block(which, g, e), kv_block(which, g, e + 1),
-                      kv_passed.at[which, g, e], kv_got.at[which, g, e + 1, 0],
+                      kv_passed.at[0], kv_got.at[which, g, e + 1],
                       (sec, 2 * right + core))
 
-    def kv_wait(g, e):
-        for which in range(2):
-            if e < 2:
-                for p in range(2):
-                    part = kv_all.at[which, g, pl.ds((reach - e) * rows + p * tok, tok)]
-                    pltpu.make_async_copy(part, part, kv_got.at[which, g, e, p]).wait()
-            else:
-                part = kv_block(which, g, e)
-                pltpu.make_async_copy(part, part, kv_got.at[which, g, e, 0]).wait()
+    def kv_wait(which, g, e):
+        part = kv_block(which, g, e)
+        pltpu.make_async_copy(part, part, kv_got.at[which, g, e]).wait()
+
+    def pass_kv(g, e):
+        with jax.named_scope('relay'):
+            for which in range(2):
+                kv_wait(which, g, e)
+                kv_relay(which, g, e).start()
 
     def qo_partner(which):
         return remote((q_in, o_in)[which].at[:, aligned(1 - core, half_feats)],
@@ -122,12 +128,28 @@
 
     w_copy = remote(wq_in, weights.at[aligned(core, feats)], w_sent.at[0], w_got.at[0], partner)
 
-    @pl.when(chip < last)
-    def _():
-        for g in range(kvh):
+    direct = reach > 1 and chips > 2
+
+    def goes_on(g, e):
+        return chip < (last - 1 if direct and g == 0 and e == 1 else last)
+
+    def send_right(g):
+        if direct and g == 0:
+            @pl.when(chip == last - 2)
+            def _():
+                for which in range(2):
+                    for p in range(2):
+                        kv_direct(which, g, p).start()
+
+        @pl.when(chip < last)
+        def _():
             for which in range(2):
                 for p in range(2):
                     kv_right(which, g, p).start()
+
+    send_right(0)
+    for g in range(1, kvh):
+        send_right(g)
 
     for g in range(kvh):
         for which in range(2):
@@ -170,14 +192,13 @@
             with jax.named_scope('bias'):
                 set_bias(blocks)
 
-    for e in range(1, reach):
-        @pl.when((chip >= e) & (chip < last))
-        def _():
-            with jax.named_scope('relay'):
-                for g in range(kvh):
-                    kv_wait(g, e)
-                    for which in range(2):
-                        kv_relay(which, g, e).start()
+    for g in range(kvh):
+        for e in range(1, reach):
+            from_chip = e if g == 0 else max(e, 2)
+
+            @pl.when((chip >= from_chip) & goes_on(g, e))
+            def _():
+                pass_kv(g, e)
 
     with jax.named_scope('qo_wait'):
         for which in range(2):
@@ -196,12 +217,12 @@
         target, piece = dq_place(unit)
         return remote(dq_buf.at[unit, p * tok:(p + 1) * tok],
                       grads.at[chip, :, aligned(piece, group * HD)],
-                      dq_sent.at[unit, p], g_got.at[chip, piece], (sec, 2 * target + p))
-
-    def dq_out(unit):
+                      dq_sent.at[0], g_got.at[chip], (sec, 2 * target + p))
+
+    def dq_out(unit, reaches=None):
         target, piece = dq_place(unit)
         for p in range(2):
-            @pl.when(2 * target + p != me)
+            @pl.when((2 * target + p != me) if reaches is None else (2 * target + p != me) & (target <= reaches))
             def _():
                 dq_copy(unit, p).start()
 
@@ -210,19 +231,40 @@
                 grads[chip, :, aligned(piece, group * HD)] = dq_buf[unit, p * tok:(p + 1) * tok]
 
     dims_last = (((1,), (1,)), ((), ()))
+
+    early = chunks * 3 // 8 if chips > 2 else 0
+
+    def far_out(first, end=chips):
+        def far_unit(n, carry):
+            unit = units - 1 - n
+            target, _ = dq_place(unit)
+
+            @pl.when((target >= first) & (target < end))
+            def _():
+                for p in range(2):
+                    dq_copy(unit, p).start()
+
+            return carry
+
+        lax.fori_loop(0, units, far_unit, 0)
+
+    held = min(2, reach)
 
     def attend(blocks):
         here = blocks * rows
         low = (reach + 1 - blocks) * rows
-        for g in range(kvh):
+        for turn in range(kvh):
+            g = jnp.where(core == 0, kvh - 1 - turn, turn) if blocks == 1 else turn
             with jax.named_scope('kv_wait'):
                 for e in range(blocks):
                     if 1 <= e < reach:
-                        @pl.when(chip == last)
+                        @pl.when(~goes_on(g, e))
                         def _():
-                            kv_wait(g, e)
+                            kv_wait(0, g, e)
+                            kv_wait(1, g, e)
                     else:
-                        kv_wait(g, e)
+                        kv_wait(0, g, e)
+                        kv_wait(1, g, e)
             k_turned[:, :here] = kv_all[0, g, low:].T
             dk_sum[:here] = jnp.zeros((here, HD), F32)
             dv_sum[:here] = jnp.zeros((here, HD), F32)
@@ -250,7 +292,12 @@
                     dq_buf[unit, :, h * HD:(h + 1) * HD] = dq.T.astype(BF16)
                 dk_sum[:here] += dk
                 dv_sum[:here] += dv
-                dq_out(unit)
+                dq_out(unit, 1 if blocks <= held else None)
+                if blocks == 2 and reach > 1 and turn + 1 < kvh:
+                    @pl.when((n == per // group // 2 - 1) & goes_on(turn + 1, 1))
+                    def _():
+                        pass_kv(turn + 1, 1)
+
                 return carry
 
             with jax.named_scope('attend'):
@@ -265,6 +312,9 @@
                             part = part * scale
                         kv_grads[e, p, :, col] = part.astype(BF16)
 
+        if blocks <= held:
+            far_out(chips // 2 + 1 if blocks == 1 and early else 2)
+
     def kvg_copy(e):
         part = kv_grads.at[e, 1 - core, :, aligned(core, span)]
         return remote(part, part, kvg_sent.at[e], kvg_got.at[e], partner)
@@ -277,8 +327,9 @@
                 kvg_copy(e).start()
 
     def kvg_wait(e):
-        part = kv_grads.at[e, core, :, aligned(1 - core, span)]
-        pltpu.make_async_copy(part, part, kvg_got.at[e]).wait()
+        with jax.named_scope('kvg_wait'):
+            part = kv_grads.at[e, core, :, aligned(1 - core, span)]
+            pltpu.make_async_copy(part, part, kvg_got.at[e]).wait()
 
     with jax.named_scope('w_wait'):
         for copy in local:
@@ -286,17 +337,9 @@
         theirs = weights.at[aligned(1 - core, feats)]
         pltpu.make_async_copy(theirs, theirs, w_got.at[0]).wait()
 
-    with jax.named_scope('kvg_wait'):
-        for e in range(reach + 1):
-            @pl.when(chip >= e)
-            def _():
-                kvg_wait(e)
-
     def grads_wait(b):
         with jax.named_scope('g_wait'):
-            for piece in range(chip_heads // group):
-                part = grads.at[b, :, piece * group * HD:(piece + 1) * group * HD]
-                pltpu.make_async_copy(part, part, g_got.at[b, piece]).wait()
+            pltpu.make_async_copy(grads.at[b], grads.at[b], g_got.at[b]).wait()
 
     for b in range(chips):
         @pl.when((chip == b) & (b // (chips // 2) != core))
@@ -305,16 +348,16 @@
 
     def right_copy(d, k):
         here = right_buf.at[d, k]
-        return remote(here, here, right_sent.at[d, k], right_got.at[d, k],
+        return remote(here, here, right_sent.at[0], right_got.at[d - 1, k],
                       (sec, jnp.minimum(me + 2, count - 2 + core)))
 
     def left_copy(d, k):
         here = left_buf.at[d, k]
-        return remote(here, here, left_sent.at[d, k], left_got.at[d, k],
+        return remote(here, here, left_sent.at[0], left_got.at[d, k],
                       (sec, jnp.maximum(me - 2, core)))
 
     def final_copy(k):
-        return remote(final.at[k], out_ref.at[:, aligned(k, cw)], final_sent.at[k], final_got.at[k],
+        return remote(final.at[k], out_ref.at[:, aligned(k, cw)], final_sent.at[0], final_got.at[k],
                       (jnp.maximum(sec - 1, 0), me))
 
     def product(d, k):
@@ -384,14 +427,14 @@
 
         lax.fori_loop(first, end, one, 0)
 
-    early = chunks * 3 // 8 if chips > 2 else 0
-    lag = 3
+    lag = 4
     leads_right = chip < chips // 2
 
     if early:
         @pl.when(chip == 0)
         def _():
             grads_wait(1)
+            far_out(2, chips // 2 + 1)
             each(0, early, lambda k: pass_right(1, k))
 
     for i in range(chips - 1):
@@ -409,6 +452,14 @@
         def _():
             grads_wait(near)
 
+        for e in range(1, reach + 1):
+            @pl.when(chip == near + e)
+            def _():
+                kvg_wait(e)
+
+        if i == min(1, chips - 2):
+            kvg_wait(0)
+
         def one(step):
             k_right = step - jnp.where(leads_right, 0, lag)
             k_left = step - jnp.where(leads_right, lag, 0)
@@ -431,63 +482,52 @@
     each(0, early, lambda k: pl.when(chip != 1)(lambda: finish(k)))
     each(early, chunks, finish)
 
-    @pl.when(chip < last)
-    def _():
-        for g in range(kvh):
-            for which in range(2):
-                for p in range(2):
-                    kv_right(which, g, p).wait_send()
-
-    for e in range(1, reach):
-        @pl.when((chip >= e) & (chip < last))
-        def _():
-            for g in range(kvh):
-                for which in range(2):
-                    kv_relay(which, g, e).wait_send()
-
-    for which in range(2):
-        for g in range(kvh):
-            kv_partner(which, g).wait_send()
-        qo_partner(which).wait_send()
-    w_copy.wait_send()
-
-    def dq_done(unit, carry):
-        target, _ = dq_place(unit)
-        for p in range(2):
-            @pl.when(2 * target + p != me)
-            def _():
-                dq_copy(unit, p).wait_send()
-        return carry
-
-    lax.fori_loop(0, own_heads // group, dq_done, 0)
-
-    for e in range(reach + 1):
-        @pl.when(chip >= e)
-        def _():
-            kvg_copy(e).wait_send()
-
-    def drain(k):
-        def right_done(i, c):
-            right_copy(last - i, k).wait_send()
-            return c
-
-        def left_done(i, c):
-            left_copy(i, k).wait_send()
-            return c
-
-        lax.fori_loop(0, last - chip, right_done, 0)
-        lax.fori_loop(0, chip, left_done, 0)
+    def sent(part, sem):
+        pltpu.make_async_copy(part, part, sem).wait()
+
+    with jax.named_scope('drain'):
+        for c in range(chips):
+            @pl.when(chip == c)
+            def _():
+                pieces = kvh * ((2 if c < last else 0) + 1) + (2 if direct and c == last - 2 else 0)
+                sent(q_all.at[:, :pieces * HD], kv_sent.at[0])
+                relays = kvh * min(c, reach - 1) if c < last else 0
+                relays -= 1 if direct and c == last - 1 else 0
+                if relays:
+                    sent(q_all.at[:, :2 * relays * HD], kv_passed.at[0])
+
+        for which in range(2):
+            qo_partner(which).wait_send()
+        w_copy.wait_send()
+
+        @pl.when(chip // (chips // 2) == core)
+        def _():
+            sent(dq_buf.at[:units - chip_heads // group // 2], dq_sent.at[0])
+
+        @pl.when(chip // (chips // 2) != core)
+        def _():
+            sent(dq_buf, dq_sent.at[0])
+
+        for e in range(reach + 1):
+            @pl.when(chip >= e)
+            def _():
+                kvg_copy(e).wait_send()
+
+        for c in range(chips):
+            @pl.when(chip == c)
+            def _():
+                if c < last:
+                    sent(right_buf.at[c + 1:], right_sent.at[0])
+                if c > 0:
+                    sent(left_buf.at[:c], left_sent.at[0])
 
         @pl.when(sec > 0)
         def _():
-            final_copy(k).wait_send()
+            sent(final, final_sent.at[0])
 
         @pl.when(sec < sections - 1)
         def _():
-            final_copy(k).wait_recv()
-
-    with jax.named_scope('drain'):
-        each(0, chunks, drain)
+            each(0, chunks, lambda k: final_copy(k).wait_recv())
 
 
 def body(queries, keys, values, out_grad, documents, query_weight, key_weight, value_weight):
@@ -503,7 +543,7 @@
     rows = 2 * tok
     reach = -(-(total // 2) // rows)
     group = 2
-    cw = min(512, width)
+    cw = min(256, width)
     chunks = width // cw
     units = chips * heads // group
     kvh = kv // 2
@@ -513,7 +553,7 @@
     vmem = pl.BlockSpec(memory_space=pltpu.VMEM)
     out = pl.pallas_call(
         functools.partial(kernel, (sections, count, tok, heads, kv, width, cw, group, reach)),
-        out_shape=jax.ShapeDtypeStruct((tok, width), BF16),
+        out_shape=pltpu.VMEM((tok, width), BF16),
         in_specs=[anywhere] * 4 + [vmem] + [anywhere] * 3,
         out_specs=vmem,
         scratch_shapes=[
@@ -535,25 +575,25 @@
             pltpu.VMEM((chunks, tok, cw), BF16),
             dma((2,)),
             dma((2, 2)),
-            dma((2, kvh, 3)),
-            dma((2, kvh, reach + 1, 2)),
+            dma((1,)),
             dma((2, kvh, reach + 1)),
+            dma((1,)),
             dma((5,)),
             dma((1,)),
             dma((1,)),
-            dma((units, 2)),
-            dma((chips, 2 * heads // group)),
+            dma((1,)),
+            dma((chips,)),
             dma((reach + 1,)),
             dma((reach + 1,)),
-            dma((chips, chunks)),
-            dma((chips, chunks)),
-            dma((chips, chunks)),
-            dma((chips, chunks)),
-            dma((chunks,)),
+            dma((1,)),
+            dma((chips - 1, chunks)),
+            dma((1,)),
+            dma((chips - 1, chunks)),
+            dma((1,)),
             dma((chunks,)),
         ],
         compiler_params=pltpu.CompilerParams(
-            collective_id=0, has_side_effects=True, vmem_limit_bytes=62 * 1024 * 1024),
+            collective_id=0, has_side_effects=True, vmem_limit_bytes=60 * 1024 * 1024),
         name="attention_back",
     )(queries[0], keys[0], values[0], out_grad[0], documents,
       query_weight[0], key_weight[0], value_weight[0])

time: 114 us -> 106 us (0.930)
  Pallas kernels: 111 us -> 105 us
  local copies, waits for them, and re-layouts: 2.29 us -> 0.97 us
    pallas_call x1, Pallas kernels: 111 us -> 105 us  [body(): pl.pallas_call(functools.partial(kernel, (sections, count, tok, heads, kv...]
    unnamed x1, local copies, waits for them, and re-layouts: 2.29 us -> 0.97 us
where the time goes in v3:
time: 106 us
  Pallas kernels  105 us (99%)
    pallas_call x1, Pallas kernels, body(): pl.pallas_call(functools.partial(kernel, (sections, count, tok, heads, kv...  105 us

profile of v3, /device:TPU:20, one launch (start us, length us, event | category | flops | bytes accessed | tf_op | source)
XLA Modules:
  0.0 105.9 jit_solution(7674883293287858891)
XLA Ops:
  0.0 104.9 %attention_back.1 = bf16[128,4096]{1,0:T(8,128)(2,1)S(1)} custom-call(bf16[128,4096]{1,0:T(8,128)(2,1)} %bitcast.12, bf16[128,512]{1,0:T(8,128)(2,1)} %bitcast.14, bf16[128,512]{1,0:T(8,128)(2,1)} %bitcast.15, bf16[128,4096]{1,0:T(8,128)(2,1)} %bitcast.13, s32[1,1024]{1,0:T(1,128)} %ids_ref.1, bf16[512,4096]{1,0:T(8,128)(2,1)} %bitcast.9, ...), custom_call_target="tpu_custom_call" | custom-call | tf_op jit(solution)/shard_map/attention_back/pallas_call | solution.py:554
  104.9 1.0 copy.10

commit v4 on v3

--- a/solution.py
+++ b/solution.py
@@ -19,9 +19,9 @@
 
 
 def kernel(dims, q_in, k_in, v_in, o_in, ids_ref, wq_in, wk_in, wv_in, out_ref,
-           q_all, o_all, kv_all, k_turned, bias, dk_sum, dv_sum, dq_buf, grads, kv_grads,
+           q_all, o_all, kv_own_all, kv_all, k_turned, bias, dk_sum, dv_sum, dq_buf, grads, kv_grads,
            weights, kv_weights, right_buf, left_buf, acc, final,
-           qo_sent, qo_got, kv_sent, kv_got, kv_passed, w_local, w_sent, w_got,
+           stage_got, qo_sent, qo_got, kv_sent, kv_got, kv_passed, w_local, w_sent, w_got,
            dq_sent, g_got, kvg_sent, kvg_got,
            right_sent, right_got, left_sent, left_got, final_sent, final_got):
     sections, count, tok, heads, kv, width, cw, group, reach = dims
@@ -45,27 +45,6 @@
     partner = (sec, me + 1 - 2 * core)
     last = chips - 1
 
-    barrier = pltpu.get_barrier_semaphore()
-
-    def greet(device):
-        pl.semaphore_signal(barrier, inc=1, device_id=device, device_id_type=MESH)
-
-    for off in range(1, count):
-        greet((sec, lax.rem(me + off, count)))
-
-    @pl.when(sec > 0)
-    def _():
-        greet((sec - 1, me))
-
-    @pl.when(sec < sections - 1)
-    def _():
-        greet((sec + 1, me))
-
-    above = jnp.where(sec > 0, 1, 0)
-    below = jnp.where(sec < sections - 1, 1, 0)
-    with jax.named_scope('barrier'):
-        pl.semaphore_wait(barrier, count - 1 + above + below)
-
     def remote(src, dst, send_sem, recv_sem, device):
         return pltpu.make_async_remote_copy(
             src_ref=src, dst_ref=dst, send_sem=send_sem, recv_sem=recv_sem,
@@ -78,17 +57,17 @@
         return pl.ds(pl.multiple_of((half * kvh + g) * HD, HD), HD)
 
     def kv_right(which, g, p):
-        return remote(kv_in[which].at[:, kv_head(p, g)],
+        return remote(kv_own_all.at[which, :, kv_head(p, g)],
                       kv_all.at[which, g, pl.ds(pl.multiple_of((reach - 1) * rows + core * tok, tok), tok)],
                       kv_sent.at[0], kv_got.at[which, g, 1], (sec, 2 * right + p))
 
     def kv_direct(which, g, p):
-        return remote(kv_in[which].at[:, kv_head(p, g)],
+        return remote(kv_own_all.at[which, :, kv_head(p, g)],
                       kv_all.at[which, g, pl.ds(pl.multiple_of((reach - 2) * rows + core * tok, tok), tok)],
                       kv_sent.at[0], kv_got.at[which, g, 2], (sec, 2 * last + p))
 
     def kv_partner(which, g):
-        return remote(kv_in[which].at[:, kv_head(1 - core, g)],
+        return remote(kv_own_all.at[which, :, kv_head(1 - core, g)],
                       kv_all.at[which, g, pl.ds(pl.multiple_of(reach * rows + core * tok, tok), tok)],
                       kv_sent.at[0], kv_got.at[which, g, 0], partner)
 
@@ -137,29 +116,25 @@
         if direct and g == 0:
             @pl.when(chip == last - 2)
             def _():
+                for p in range(2):
+                    for which in range(2):
+                        kv_direct(which, g, p).start()
+
+        @pl.when(chip < last)
+        def _():
+            for p in range(2):
                 for which in range(2):
-                    for p in range(2):
-                        kv_direct(which, g, p).start()
-
-        @pl.when(chip < last)
-        def _():
-            for which in range(2):
-                for p in range(2):
                     kv_right(which, g, p).start()
 
-    send_right(0)
-    for g in range(1, kvh):
-        send_right(g)
-
+    staged = [pltpu.make_async_copy(kv_in[which], kv_own_all.at[which], stage_got.at[which])
+              for which in range(2)]
+    for copy in staged:
+        copy.start()
+    for which in range(2):
+        qo_own(which).start()
     for g in range(kvh):
         for which in range(2):
             kv_own(which, g).start()
-            kv_partner(which, g).start()
-    for which in range(2):
-        qo_own(which).start()
-        qo_partner(which).start()
-
-    w_copy.start()
     local = [pltpu.make_async_copy(wq_in, weights.at[aligned(core, feats)], w_local.at[0])]
     for r in range(2):
         part = slice(r * kvh * HD, (r + 1) * kvh * HD)
@@ -168,6 +143,41 @@
             local.append(pltpu.make_async_copy(
                 source.at[part], kv_weights.at[base:base + kvh * HD],
                 w_local.at[1 + 2 * r + which]))
+    barrier = pltpu.get_barrier_semaphore()
+
+    def greet(device):
+        pl.semaphore_signal(barrier, inc=1, device_id=device, device_id_type=MESH)
+
+    for off in range(1, count):
+        greet((sec, lax.rem(me + off, count)))
+
+    @pl.when(sec > 0)
+    def _():
+        greet((sec - 1, me))
+
+    @pl.when(sec < sections - 1)
+    def _():
+        greet((sec + 1, me))
+
+    above = jnp.where(sec > 0, 1, 0)
+    below = jnp.where(sec < sections - 1, 1, 0)
+    with jax.named_scope('barrier'):
+        pl.semaphore_wait(barrier, count - 1 + above + below)
+
+    for copy in staged:
+        copy.wait()
+
+    send_right(0)
+    for g in range(1, kvh):
+        send_right(g)
+
+    for g in range(kvh):
+        for which in range(2):
+            kv_partner(which, g).start()
+    for which in range(2):
+        qo_partner(which).start()
+
+    w_copy.start()
     for copy in local:
         copy.start()
 
@@ -232,7 +242,8 @@
 
     dims_last = (((1,), (1,)), ((), ()))
 
-    early = chunks * 3 // 8 if chips > 2 else 0
+    early = chunks * 3 // 8 if chips > 3 else 0
+    early_left = chunks // 4 if chips > 3 else 0
 
     def far_out(first, end=chips):
         def far_unit(n, carry):
@@ -249,6 +260,7 @@
         lax.fori_loop(0, units, far_unit, 0)
 
     held = min(2, reach)
+    batch = 1
 
     def attend(blocks):
         here = blocks * rows
@@ -269,39 +281,54 @@
             dk_sum[:here] = jnp.zeros((here, HD), F32)
             dv_sum[:here] = jnp.zeros((here, HD), F32)
 
-            def one_unit(n, carry):
-                unit = g * (per // group) + n
+            def unit_of(n, h):
+                return g * (per // group) + n * batch + h // group
+
+            def one_batch(n, carry):
                 dk = jnp.zeros((here, HD), F32)
                 dv = jnp.zeros((here, HD), F32)
-                for h in range(group):
-                    col = aligned(unit * group + h, HD)
-                    q = q_all[:, col]
-                    o = o_all[:, col]
-                    s = lax.dot_general(kv_all[0, g, low:], q, dims_last, preferred_element_type=F32)
-                    dp = lax.dot_general(kv_all[1, g, low:], o, dims_last, preferred_element_type=F32)
-                    s = s + bias[:here]
+                heads_here = range(batch * group)
+                cols = [aligned(unit_of(n, h) * group + h % group, HD) for h in heads_here]
+                scores, dprobs = {}, {}
+
+                def start_head(h):
+                    scores[h] = lax.dot_general(kv_all[0, g, low:], q_all[:, cols[h]], dims_last,
+                                                preferred_element_type=F32) + bias[:here]
+                    dprobs[h] = lax.dot_general(kv_all[1, g, low:], o_all[:, cols[h]], dims_last,
+                                                preferred_element_type=F32)
+
+                def weigh(h):
+                    s, dp = scores.pop(h), dprobs.pop(h)
                     top = jnp.max(s, axis=0, keepdims=True)
                     e = jnp.exp2((s - top) * to_log2)
                     inv = 1.0 / jnp.sum(e, axis=0, keepdims=True)
                     delta = jnp.sum(e * dp, axis=0, keepdims=True) * inv
                     prob = e * inv
-                    ds = (prob * (dp - delta)).astype(BF16)
-                    dv += jnp.dot(prob.astype(BF16), o, preferred_element_type=F32)
-                    dk += jnp.dot(ds, q, preferred_element_type=F32)
+                    return prob.astype(BF16), (prob * (dp - delta)).astype(BF16)
+
+                start_head(0)
+                for h in heads_here:
+                    if h + 1 < len(heads_here):
+                        start_head(h + 1)
+                    prob, ds = weigh(h)
+                    dv += jnp.dot(prob, o_all[:, cols[h]], preferred_element_type=F32)
+                    dk += jnp.dot(ds, q_all[:, cols[h]], preferred_element_type=F32)
                     dq = jnp.dot(k_turned[:, :here], ds, preferred_element_type=F32) * scale
-                    dq_buf[unit, :, h * HD:(h + 1) * HD] = dq.T.astype(BF16)
+                    at = h % group
+                    dq_buf[unit_of(n, h), :, at * HD:(at + 1) * HD] = dq.T.astype(BF16)
+                if at == group - 1:
+                        dq_out(unit_of(n, h), 1 if blocks <= held else None)
                 dk_sum[:here] += dk
                 dv_sum[:here] += dv
-                dq_out(unit, 1 if blocks <= held else None)
                 if blocks == 2 and reach > 1 and turn + 1 < kvh:
-                    @pl.when((n == per // group // 2 - 1) & goes_on(turn + 1, 1))
+                    @pl.when((n == per // group // batch // 2 - 1) & goes_on(turn + 1, 1))
                     def _():
                         pass_kv(turn + 1, 1)
 
                 return carry
 
             with jax.named_scope('attend'):
-                lax.fori_loop(0, per // group, one_unit, 0)
+                lax.fori_loop(0, per // group // batch, one_batch, 0)
             for e in range(blocks):
                 at = (blocks - 1 - e) * rows
                 for which, sums in enumerate((dk_sum, dv_sum)):
@@ -341,11 +368,6 @@
         with jax.named_scope('g_wait'):
             pltpu.make_async_copy(grads.at[b], grads.at[b], g_got.at[b]).wait()
 
-    for b in range(chips):
-        @pl.when((chip == b) & (b // (chips // 2) != core))
-        def _():
-            grads_wait(b)
-
     def right_copy(d, k):
         here = right_buf.at[d, k]
         return remote(here, here, right_sent.at[0], right_got.at[d - 1, k],
@@ -442,23 +464,36 @@
         to_right = chip < far
         to_left = chip > near
         begin = early if i == chips - 2 else 0
+        begin_left = early_left if i == chips - 2 else 0
+
+        if early_left and i == chips - 3:
+            @pl.when(chip == last)
+            def _():
+                grads_wait(chips - 2)
+                kvg_wait(1)
+                each(0, early_left, lambda k: pass_left(chips - 2, k))
 
         @pl.when(to_right)
         def _():
             if begin == 0:
                 grads_wait(far)
 
-        @pl.when(to_left)
-        def _():
-            grads_wait(near)
-
-        for e in range(1, reach + 1):
-            @pl.when(chip == near + e)
-            def _():
-                kvg_wait(e)
+        if begin_left == 0:
+            @pl.when(to_left)
+            def _():
+                grads_wait(near)
+
+            for e in range(1, reach + 1):
+                @pl.when(chip == near + e)
+                def _():
+                    kvg_wait(e)
 
         if i == min(1, chips - 2):
             kvg_wait(0)
+            for b in range(chips):
+                @pl.when((chip == b) & (b // (chips // 2) != core))
+                def _():
+                    grads_wait(b)
 
         def one(step):
             k_right = step - jnp.where(leads_right, 0, lag)
@@ -468,7 +503,7 @@
             def _():
                 pass_right(far, k_right)
 
-            @pl.when(to_left & (k_left >= 0) & (k_left < chunks))
+            @pl.when(to_left & (k_left >= begin_left) & (k_left < chunks))
             def _():
                 pass_left(near, k_left)
 
@@ -477,10 +512,15 @@
                 def _():
                     finish(k_left)
 
+            if early_left and i == chips - 3:
+                @pl.when((chip == chips - 2) & (k_right >= 0) & (k_right < early_left))
+                def _():
+                    finish(k_right)
+
         each(0, chunks + lag, one)
 
-    each(0, early, lambda k: pl.when(chip != 1)(lambda: finish(k)))
-    each(early, chunks, finish)
+    done = jnp.where(chip == chips - 2, early_left, 0)
+    each(jnp.where(chip == 1, early, done), chunks, finish)
 
     def sent(part, sem):
         pltpu.make_async_copy(part, part, sem).wait()
@@ -559,6 +599,7 @@
         scratch_shapes=[
             pltpu.VMEM((rows, chips * feats), BF16),
             pltpu.VMEM((rows, chips * feats), BF16),
+            pltpu.VMEM((2, tok, kv * HD), BF16),
             pltpu.VMEM((2, kvh, slots, HD), BF16),
             pltpu.VMEM((HD, slots), BF16),
             pltpu.VMEM((slots, rows), F32),
@@ -574,6 +615,7 @@
             pltpu.VMEM((tok, cw), F32),
             pltpu.VMEM((chunks, tok, cw), BF16),
             dma((2,)),
+            dma((2,)),
             dma((2, 2)),
             dma((1,)),
             dma((2, kvh, reach + 1)),

time: 106 us -> 105 us (level)
  Pallas kernels: 105 us -> 103 us
    pallas_call x1, Pallas kernels: 105 us -> 103 us  [body(): pl.pallas_call(functools.partial(kernel, (sections, count, tok, heads, kv...]
where the time goes in v4:
time: 105 us; the launch traced here: 104 us
  Pallas kernels  103 us (98%)
    pallas_call x1, Pallas kernels, body(): pl.pallas_call(functools.partial(kernel, (sections, count, tok, heads, kv...  103 us

profile of v4, /device:TPU:20, one launch (start us, length us, event | category | flops | bytes accessed | tf_op | source)
XLA Modules:
  0.0 104.3 jit_solution(6367544798659050173)
XLA Ops:
  0.0 103.4 %attention_back.1 = bf16[128,4096]{1,0:T(8,128)(2,1)S(1)} custom-call(bf16[128,4096]{1,0:T(8,128)(2,1)} %bitcast.12, bf16[128,512]{1,0:T(8,128)(2,1)} %bitcast.14, bf16[128,512]{1,0:T(8,128)(2,1)} %bitcast.15, bf16[128,4096]{1,0:T(8,128)(2,1)} %bitcast.13, s32[1,1024]{1,0:T(1,128)} %ids_ref.1, bf16[512,4096]{1,0:T(8,128)(2,1)} %bitcast.9, ...), custom_call_target="tpu_custom_call" | custom-call | tf_op jit(solution)/shard_map/attention_back/pallas_call | solution.py:594
  103.4 1.0 copy.10

commit v5 on v4

--- a/solution.py
+++ b/solution.py
@@ -18,10 +18,10 @@
     return pl.ds(pl.multiple_of(index * size, size), size)
 
 
-def kernel(dims, q_in, k_in, v_in, o_in, ids_ref, wq_in, wk_in, wv_in, out_ref,
-           q_all, o_all, kv_own_all, kv_all, k_turned, bias, dk_sum, dv_sum, dq_buf, grads, kv_grads,
+def kernel(dims, q_in, k_in, v_in, o_in, ids_in, wq_in, wk_in, wv_in, out_ref,
+           ids_ref, q_all, o_all, kv_own_all, kv_all, k_turned, bias, dk_sum, dv_sum, dq_buf, grads, kv_grads,
            weights, kv_weights, right_buf, left_buf, acc, final,
-           stage_got, qo_sent, qo_got, kv_sent, kv_got, kv_passed, w_local, w_sent, w_got,
+           ids_got, stage_got, qo_sent, qo_got, kv_sent, kv_got, kv_passed, w_local, w_sent, w_got,
            dq_sent, g_got, kvg_sent, kvg_got,
            right_sent, right_got, left_sent, left_got, final_sent, final_got):
     sections, count, tok, heads, kv, width, cw, group, reach = dims
@@ -128,7 +128,8 @@
 
     staged = [pltpu.make_async_copy(kv_in[which], kv_own_all.at[which], stage_got.at[which])
               for which in range(2)]
-    for copy in staged:
+    ids_copy = pltpu.make_async_copy(ids_in, ids_ref, ids_got.at[0])
+    for copy in staged + [ids_copy]:
         copy.start()
     for which in range(2):
         qo_own(which).start()
@@ -185,6 +186,7 @@
     def _():
         out_ref[...] = jnp.zeros_like(out_ref)
 
+    ids_copy.wait()
     q_ids = ids_ref[:, aligned(chip, rows)]
 
     def set_bias(blocks):
@@ -594,9 +596,10 @@
     out = pl.pallas_call(
         functools.partial(kernel, (sections, count, tok, heads, kv, width, cw, group, reach)),
         out_shape=pltpu.VMEM((tok, width), BF16),
-        in_specs=[anywhere] * 4 + [vmem] + [anywhere] * 3,
+        in_specs=[anywhere] * 8,
         out_specs=vmem,
         scratch_shapes=[
+            pltpu.VMEM((1, total), jnp.int32),
             pltpu.VMEM((rows, chips * feats), BF16),
             pltpu.VMEM((rows, chips * feats), BF16),
             pltpu.VMEM((2, tok, kv * HD), BF16),
@@ -614,6 +617,7 @@
             pltpu.VMEM((chips, chunks, tok, cw), BF16),
             pltpu.VMEM((tok, cw), F32),
             pltpu.VMEM((chunks, tok, cw), BF16),
+            dma((1,)),
             dma((2,)),
             dma((2,)),
             dma((2, 2)),

time: 105 us -> 104 us (level)
  no operation moved by 1% of the time
where the time goes in v5:
time: 104 us
  Pallas kernels  103 us (99%)
    pallas_call x1, Pallas kernels, body(): pl.pallas_call(functools.partial(kernel, (sections, count, tok, heads, kv...  103 us

profile of v5, /device:TPU:20, one launch (start us, length us, event | category | flops | bytes accessed | tf_op | source)
XLA Modules:
  0.0 103.7 jit_solution(12120008386116580816)
XLA Ops:
  0.0 102.7 %attention_back.1 = bf16[128,4096]{1,0:T(8,128)(2,1)S(1)} custom-call(bf16[128,4096]{1,0:T(8,128)(2,1)} %bitcast.12, bf16[128,512]{1,0:T(8,128)(2,1)} %bitcast.14, bf16[128,512]{1,0:T(8,128)(2,1)} %bitcast.15, bf16[128,4096]{1,0:T(8,128)(2,1)} %bitcast.13, s32[1,1024]{1,0:T(1,128)} %ids_in.1, bf16[512,4096]{1,0:T(8,128)(2,1)} %bitcast.9, ...), custom_call_target="tpu_custom_call" | custom-call | tf_op jit(solution)/shard_map/attention_back/pallas_call | solution.py:596
  102.7 1.0 copy.10

commit v6 on v5

--- a/solution.py
+++ b/solution.py
@@ -23,7 +23,7 @@
            weights, kv_weights, right_buf, left_buf, acc, final,
            ids_got, stage_got, qo_sent, qo_got, kv_sent, kv_got, kv_passed, w_local, w_sent, w_got,
            dq_sent, g_got, kvg_sent, kvg_got,
-           right_sent, right_got, left_sent, left_got, final_sent, final_got):
+           right_sent, right_got, left_sent, left_got, near_got, half_got, final_sent, final_got):
     sections, count, tok, heads, kv, width, cw, group, reach = dims
     chips = count // 2
     rows = 2 * tok
@@ -98,12 +98,12 @@
     def qo_partner(which):
         return remote((q_in, o_in)[which].at[:, aligned(1 - core, half_feats)],
                       (q_all, o_all)[which].at[aligned(core, tok)],
-                      qo_sent.at[which], qo_got.at[which, 0], partner)
+                      qo_sent.at[which], qo_got.at[which], partner)
 
     def qo_own(which):
         return pltpu.make_async_copy((q_in, o_in)[which].at[:, aligned(core, half_feats)],
                                      (q_all, o_all)[which].at[aligned(core, tok)],
-                                     qo_got.at[which, 1])
+                                     qo_got.at[which])
 
     w_copy = remote(wq_in, weights.at[aligned(core, feats)], w_sent.at[0], w_got.at[0], partner)
 
@@ -143,7 +143,7 @@
             base = r * span + which * kvh * HD
             local.append(pltpu.make_async_copy(
                 source.at[part], kv_weights.at[base:base + kvh * HD],
-                w_local.at[1 + 2 * r + which]))
+                w_local.at[1]))
     barrier = pltpu.get_barrier_semaphore()
 
     def greet(device):
@@ -215,9 +215,7 @@
     with jax.named_scope('qo_wait'):
         for which in range(2):
             buf = (q_all, o_all)[which]
-            qo_own(which).wait()
-            part = buf.at[aligned(1 - core, tok)]
-            pltpu.make_async_copy(part, part, qo_got.at[which, 0]).wait()
+            pltpu.make_async_copy(buf, buf, qo_got.at[which]).wait()
 
     def dq_place(unit):
         head = unit * group
@@ -244,8 +242,8 @@
 
     dims_last = (((1,), (1,)), ((), ()))
 
-    early = chunks * 3 // 8 if chips > 3 else 0
-    early_left = chunks // 4 if chips > 3 else 0
+    early = chunks * 3 // 16 * 2 if chips > 3 else 0
+    early_left = chunks // 8 * 2 if chips > 3 else 0
 
     def far_out(first, end=chips):
         def far_unit(n, carry):
@@ -361,8 +359,8 @@
             pltpu.make_async_copy(part, part, kvg_got.at[e]).wait()
 
     with jax.named_scope('w_wait'):
-        for copy in local:
-            copy.wait()
+        local[0].wait()
+        pltpu.make_async_copy(kv_weights, kv_weights, w_local.at[1]).wait()
         theirs = weights.at[aligned(1 - core, feats)]
         pltpu.make_async_copy(theirs, theirs, w_got.at[0]).wait()
 
@@ -370,19 +368,52 @@
         with jax.named_scope('g_wait'):
             pltpu.make_async_copy(grads.at[b], grads.at[b], g_got.at[b]).wait()
 
-    def right_copy(d, k):
-        here = right_buf.at[d, k]
-        return remote(here, here, right_sent.at[0], right_got.at[d - 1, k],
-                      (sec, jnp.minimum(me + 2, count - 2 + core)))
-
-    def left_copy(d, k):
-        here = left_buf.at[d, k]
-        return remote(here, here, left_sent.at[0], left_got.at[d, k],
-                      (sec, jnp.maximum(me - 2, core)))
+    tail = chunks - 1
+    half = cw // 2
+
+    def right_target(section):
+        return (section, jnp.minimum(me + 2, count - 2 + core))
+
+    def left_target(section):
+        return (section, jnp.maximum(me - 2, core))
+
+    def start_one(buf, sent_sem, sem, d, k, target, beside):
+        if d != beside:
+            here = buf.at[d, k]
+            remote(here, here, sent_sem.at[0], sem(d, k), target).start()
+            return
+
+        @pl.when(k < tail)
+        def _():
+            here = buf.at[d, k]
+            remote(here, here, sent_sem.at[0], near_got.at[k], target).start()
+
+        @pl.when(k == tail)
+        def _():
+            for h in range(2):
+                here = buf.at[d, tail, :, h * half:(h + 1) * half]
+                remote(here, here, sent_sem.at[0], half_got.at[0] if h else near_got.at[tail], target).start()
+
+    def right_sem(d, k):
+        return right_got.at[d - 2, k]
+
+    def left_sem(d, k):
+        return left_got.at[d, k]
+
+    def got(part, sem):
+        pltpu.make_async_copy(part, part, sem).wait()
+
+    before = jnp.maximum(sec - 1, 0)
+    is_beside = (chip == 1) | (chip == chips - 2)
 
     def final_copy(k):
-        return remote(final.at[k], out_ref.at[:, aligned(k, cw)], final_sent.at[0], final_got.at[k],
-                      (jnp.maximum(sec - 1, 0), me))
+        return remote(final.at[k], out_ref.at[:, aligned(k, cw)], final_sent.at[0], final_got.at[0],
+                      (before, me))
+
+    def final_half(h):
+        return remote(final.at[tail, :, h * half:(h + 1) * half],
+                      out_ref.at[:, tail * cw + h * half:tail * cw + (h + 1) * half],
+                      final_sent.at[0], final_got.at[0], (before, me))
 
     def product(d, k):
         acc[...] = jnp.dot(grads[d], weights[:, aligned(k, cw)], preferred_element_type=F32)
@@ -395,14 +426,15 @@
         with jax.named_scope('r_prod'):
             product(d, k)
 
-        @pl.when(chip > 0)
-        def _():
-            with jax.named_scope('r_wait'):
-                right_copy(d, k).wait_recv()
-            acc[...] += right_buf[d, k].astype(F32)
+        if d > 1:
+            @pl.when(chip > 0)
+            def _():
+                with jax.named_scope('r_wait'):
+                    got(right_buf.at[d, k], right_sem(d, k))
+                acc[...] += right_buf[d, k].astype(F32)
 
         right_buf[d, k] = acc[...].astype(BF16)
-        right_copy(d, k).start()
+        start_one(right_buf, right_sent, right_sem, d, k, right_target(sec), 1)
 
     def pass_left(d, k):
         with jax.named_scope('l_prod'):
@@ -412,37 +444,63 @@
             def _():
                 kv_product(jnp.minimum(chip - d, reach), k)
 
-        @pl.when(chip < last)
-        def _():
-            with jax.named_scope('l_wait'):
-                left_copy(d, k).wait_recv()
-            acc[...] += left_buf[d, k].astype(F32)
+        if d < chips - 2:
+            @pl.when(chip < last)
+            def _():
+                with jax.named_scope('l_wait'):
+                    got(left_buf.at[d, k], left_sem(d, k))
+                acc[...] += left_buf[d, k].astype(F32)
 
         left_buf[d, k] = acc[...].astype(BF16)
-        left_copy(d, k).start()
+        start_one(left_buf, left_sent, left_sem, d, k, left_target(sec), chips - 2)
 
     def finish(k):
         with jax.named_scope('f_prod'):
             product(chip, k)
             kv_product(0, k)
 
-        @pl.when(chip > 0)
+        @pl.when(chip > 1)
         def _():
             with jax.named_scope('f_wait_r'):
-                right_copy(chip, k).wait_recv()
+                got(right_buf.at[chip, k], right_sem(chip, k))
             acc[...] += right_buf[chip, k].astype(F32)
 
-        @pl.when(chip < last)
+        @pl.when(chip < chips - 2)
         def _():
             with jax.named_scope('f_wait_l'):
-                left_copy(chip, k).wait_recv()
+                got(left_buf.at[chip, k], left_sem(chip, k))
             acc[...] += left_buf[chip, k].astype(F32)
 
-        final[k] = acc[...].astype(BF16)
-
-        @pl.when(sec > 0)
-        def _():
-            final_copy(k).start()
+        for beside, buf in ((1, right_buf), (chips - 2, left_buf)):
+            @pl.when((chip == beside) & (k < tail))
+            def _():
+                with jax.named_scope('f_wait_n'):
+                    got(buf.at[beside, k], near_got.at[k])
+                acc[...] += buf[beside, k].astype(F32)
+
+        @pl.when(~is_beside | (k < tail))
+        def _():
+            final[k] = acc[...].astype(BF16)
+
+            @pl.when(sec > 0)
+            def _():
+                final_copy(k).start()
+
+        @pl.when(is_beside & (k == tail))
+        def _():
+            for h in range(2):
+                cols = slice(h * half, (h + 1) * half)
+                for beside, buf in ((1, right_buf), (chips - 2, left_buf)):
+                    @pl.when(chip == beside)
+                    def _():
+                        got(buf.at[beside, tail, :, cols], half_got.at[0] if h else near_got.at[tail])
+                        acc[:, cols] += buf[beside, tail, :, cols].astype(F32)
+
+                final[tail, :, cols] = acc[:, cols].astype(BF16)
+
+                @pl.when(sec > 0)
+                def _():
+                    final_half(h).start()
 
     def each(first, end, act):
         def one(k, carry):
@@ -569,7 +627,7 @@
 
         @pl.when(sec < sections - 1)
         def _():
-            each(0, chunks, lambda k: final_copy(k).wait_recv())
+            got(final, final_got.at[0])
 
 
 def body(queries, keys, values, out_grad, documents, query_weight, key_weight, value_weight):
@@ -620,11 +678,11 @@
             dma((1,)),
             dma((2,)),
             dma((2,)),
-            dma((2, 2)),
+            dma((2,)),
             dma((1,)),
             dma((2, kvh, reach + 1)),
             dma((1,)),
-            dma((5,)),
+            dma((2,)),
             dma((1,)),
             dma((1,)),
             dma((1,)),
@@ -632,11 +690,13 @@
             dma((reach + 1,)),
             dma((reach + 1,)),
             dma((1,)),
-            dma((chips - 1, chunks)),
-            dma((1,)),
-            dma((chips - 1, chunks)),
-            dma((1,)),
+            dma((max(chips - 2, 1), chunks)),
+            dma((1,)),
+            dma((max(chips - 2, 1), chunks)),
             dma((chunks,)),
+            dma((1,)),
+            dma((1,)),
+            dma((1,)),
         ],
         compiler_params=pltpu.CompilerParams(
             collective_id=0, has_side_effects=True, vmem_limit_bytes=60 * 1024 * 1024),

time: 104 us -> 104 us (level)
  no operation moved by 1% of the time
where the time goes in v6:
time: 104 us; the launch traced here: 103 us
  Pallas kernels  102 us (98%)
    pallas_call x1, Pallas kernels, body(): pl.pallas_call(functools.partial(kernel, (sections, count, tok, heads, kv...  102 us

profile of v6, /device:TPU:20, one launch (start us, length us, event | category | flops | bytes accessed | tf_op | source)
XLA Modules:
  0.0 103.4 jit_solution(17558739929729704531)
XLA Ops:
  0.0 102.4 %attention_back.1 = bf16[128,4096]{1,0:T(8,128)(2,1)S(1)} custom-call(bf16[128,4096]{1,0:T(8,128)(2,1)} %bitcast.12, bf16[128,512]{1,0:T(8,128)(2,1)} %bitcast.14, bf16[128,512]{1,0:T(8,128)(2,1)} %bitcast.15, bf16[128,4096]{1,0:T(8,128)(2,1)} %bitcast.13, s32[1,1024]{1,0:T(1,128)} %ids_in.1, bf16[512,4096]{1,0:T(8,128)(2,1)} %bitcast.9, ...), custom_call_target="tpu_custom_call" | custom-call | tf_op jit(solution)/shard_map/attention_back/pallas_call | solution.py:654
  102.4 1.0 copy.10

commit v7 on v6

--- a/solution.py
+++ b/solution.py
@@ -182,10 +182,6 @@
     for copy in local:
         copy.start()
 
-    @pl.when(sec == sections - 1)
-    def _():
-        out_ref[...] = jnp.zeros_like(out_ref)
-
     ids_copy.wait()
     q_ids = ids_ref[:, aligned(chip, rows)]
 
@@ -243,7 +239,7 @@
     dims_last = (((1,), (1,)), ((), ()))
 
     early = chunks * 3 // 16 * 2 if chips > 3 else 0
-    early_left = chunks // 8 * 2 if chips > 3 else 0
+    early_left = chunks // 2 if chips > 3 else 0
 
     def far_out(first, end=chips):
         def far_unit(n, carry):
@@ -316,8 +312,7 @@
                     dq = jnp.dot(k_turned[:, :here], ds, preferred_element_type=F32) * scale
                     at = h % group
                     dq_buf[unit_of(n, h), :, at * HD:(at + 1) * HD] = dq.T.astype(BF16)
-                if at == group - 1:
-                        dq_out(unit_of(n, h), 1 if blocks <= held else None)
+                dq_out(unit_of(n, 0), 1 if blocks <= held else None)
                 dk_sum[:here] += dk
                 dv_sum[:here] += dv
                 if blocks == 2 and reach > 1 and turn + 1 < kvh:
@@ -581,6 +576,10 @@
 
     done = jnp.where(chip == chips - 2, early_left, 0)
     each(jnp.where(chip == 1, early, done), chunks, finish)
+
+    @pl.when(sec == sections - 1)
+    def _():
+        out_ref[...] = jnp.zeros_like(out_ref)
 
     def sent(part, sem):
         pltpu.make_async_copy(part, part, sem).wait()

time: 104 us -> 104 us (level)
  no operation moved by 1% of the time
where the time goes in v7:
time: 104 us; the launch traced here: 103 us
  Pallas kernels  102 us (98%)
    pallas_call x1, Pallas kernels, body(): pl.pallas_call(functools.partial(kernel, (sections, count, tok, heads, kv...  102 us

profile of v7, /device:TPU:20, one launch (start us, length us, event | category | flops | bytes accessed | tf_op | source)
XLA Modules:
  0.0 103.4 jit_solution(15378446932311605618)
XLA Ops:
  0.0 102.4 %attention_back.1 = bf16[128,4096]{1,0:T(8,128)(2,1)S(1)} custom-call(bf16[128,4096]{1,0:T(8,128)(2,1)} %bitcast.12, bf16[128,512]{1,0:T(8,128)(2,1)} %bitcast.14, bf16[128,512]{1,0:T(8,128)(2,1)} %bitcast.15, bf16[128,4096]{1,0:T(8,128)(2,1)} %bitcast.13, s32[1,1024]{1,0:T(1,128)} %ids_in.1, bf16[512,4096]{1,0:T(8,128)(2,1)} %bitcast.9, ...), custom_call_target="tpu_custom_call" | custom-call | tf_op jit(solution)/shard_map/attention_back/pallas_call | solution.py:653
  102.4 1.0 copy.10
